TPU v7x, 32 devices: a whole 2x2x4 slice. The times are simulated.
32 devices in a mesh: groups: 2 (over y), tp: 4 (over x, core), sp: 4 (over z).
Axes of the slice: x: 2, y: 2, z: 4, core: 2. Of those that a mesh axis runs over, the one named last changes fastest.
Arguments:
- query_rows: bfloat16 [4, 128, 4096], P('groups', ('sp', 'tp')), parts along dimension 0, may hold values from -100 to 100
- key_rows: bfloat16 [4, 128, 4096], P('groups', ('sp', 'tp')), parts along dimension 0, may hold values from -4 to 4
- value_rows: bfloat16 [4, 128, 4096], P('groups', ('sp', 'tp')), parts along dimension 0, may hold values from -6 to 6
- residual: bfloat16 [4, 128, 2560], P('groups', 'sp', 'tp'), parts along dimension 0, may hold values from -100 to 100
- modulation: float32 [4, 2560], P(None, 'tp'), may hold values from -3 to 3
- out_weight: bfloat16 [2560, 4096], P('tp', 'sp'), may hold values from -0.375 to 0.375
- up_weight: bfloat16 [2560, 7168], P('sp', 'tp'), may hold values from -0.125 to 0.125
- down_weight: bfloat16 [2560, 7168], P('sp', 'tp'), may hold values from -0.0625 to 0.0625
Outputs:
- block_out: bfloat16 [4, 128, 2560], P('groups', 'sp', 'tp'), parts along dimension 0
There are 2 independent parts, one for each index of `groups`. A program takes and returns all parts, laid end to end along the dimension named above; an argument that names none is the same for every part. Nothing has to cross between parts.
All inputs are finite; a program needn't handle non-finite values.
Results may differ from a plain program's by a relative error of at most 0.0044.
Values may be sent and summed in bfloat16 or wider, within the bound.
A program may use at most 64 MiB of HBM per device.

v0:
```python
import math

import jax
import jax.numpy as jnp
from jax import lax
from jax.sharding import PartitionSpec as P

D = 2560
HEAD_FEATURES = 128


def contract_last(left, right):
    return lax.dot_general(
        left, right, (((1,), (1,)), ((), ())), preferred_element_type=jnp.float32
    )


def attend(query_part, key_part, value_part):
    query_heads, key_heads, value_heads = (
        lax.all_to_all(query_part, "sp", split_axis=2, concat_axis=1, tiled=True),
        lax.all_to_all(key_part, "sp", split_axis=2, concat_axis=1, tiled=True),
        lax.all_to_all(value_part, "sp", split_axis=2, concat_axis=1, tiled=True),
    )
    batches, query_count, local_width = query_heads.shape
    local_heads = local_width // HEAD_FEATURES
    grouped = query_heads.reshape(batches, query_count, local_heads, HEAD_FEATURES)
    score_scale = 1.0 / math.sqrt(HEAD_FEATURES)

    def absorb_block(running, blocks):
        block_keys, block_values = blocks
        highest, row_total, weighted_values = running
        attention_logits = (
            jnp.einsum("bqhd,bkhd->bqhk", grouped, block_keys, preferred_element_type=jnp.float32)
            * score_scale
        )
        raised = jnp.maximum(highest, jnp.max(attention_logits, axis=-1))
        damping = jnp.exp(highest - raised)
        exponent = jnp.exp(attention_logits - raised[..., None])
        row_total = row_total * damping + jnp.sum(exponent, axis=-1)
        weighted_values = weighted_values * damping[..., None] + jnp.einsum(
            "bqhk,bkhd->bqhd",
            exponent.astype(jnp.bfloat16),
            block_values,
            preferred_element_type=jnp.float32,
        )
        return (raised, row_total, weighted_values)

    def scan_step(running, blocks):
        return (absorb_block(running, blocks), None)

    def absorb(running, section):
        key_section, value_section = section
        key_count = key_section.shape[1]
        shaped_keys = key_section.reshape(batches, key_count, local_heads, HEAD_FEATURES)
        shaped_values = value_section.reshape(batches, key_count, local_heads, HEAD_FEATURES)
        if key_count > 512 and key_count % 512 == 0:
            block_count = key_count // 512
            key_blocks = jnp.moveaxis(
                shaped_keys.reshape(batches, block_count, 512, local_heads, HEAD_FEATURES), 1, 0
            )
            value_blocks = jnp.moveaxis(
                shaped_values.reshape(batches, block_count, 512, local_heads, HEAD_FEATURES), 1, 0
            )
            running, unused = lax.scan(scan_step, running, (key_blocks, value_blocks))
            return running
        return absorb_block(running, (shaped_keys, shaped_values))

    starting = (
        jnp.full((batches, query_count, local_heads), -jnp.inf, jnp.float32),
        jnp.zeros((batches, query_count, local_heads), jnp.float32),
        jnp.zeros((batches, query_count, local_heads, HEAD_FEATURES), jnp.float32),
    )
    highest, row_total, weighted_values = absorb(
        starting,
        (
            lax.all_gather(key_heads, "tp", axis=1, tiled=True),
            lax.all_gather(value_heads, "tp", axis=1, tiled=True),
        ),
    )
    normalized = (weighted_values / row_total[..., None]).astype(jnp.bfloat16)
    ordered = normalized.reshape(batches, query_count, local_width)
    return lax.all_to_all(ordered, "sp", split_axis=1, concat_axis=2, tiled=True)


def body(
    query_rows, key_rows, value_rows, residual, modulation, out_weight, up_weight, down_weight
):
    attended = attend(query_rows, key_rows, value_rows)
    stripes = lax.all_gather(attended, "tp", axis=1, tiled=True)
    batches, rows_block, inner_width = stripes.shape
    row_count = batches * rows_block
    flat_rows = stripes.reshape(row_count, inner_width)
    local_width = out_weight.shape[0]
    columns = flat_rows
    projected = contract_last(columns, lax.all_gather(out_weight, "sp", axis=1, tiled=True))
    mixed_rows = (
        residual.reshape(row_count, local_width).astype(jnp.float32) + modulation[0] * projected
    )
    first_sum, second_sum = lax.psum(
        (jnp.sum(mixed_rows, axis=1), jnp.sum(mixed_rows * mixed_rows, axis=1)), "tp"
    )
    row_mean = first_sum / D
    spread = second_sum / D - row_mean * row_mean
    normed = (
        (mixed_rows - row_mean[:, None])
        * lax.rsqrt(spread[:, None] + 1e-06)
        * (1.0 + modulation[2])
        + modulation[1]
    ).astype(jnp.bfloat16)
    gathered = lax.all_gather(normed, "tp", axis=1, tiled=True)
    columns = gathered
    hidden = jnp.dot(
        columns,
        lax.all_gather(up_weight, "sp", axis=0, tiled=True),
        preferred_element_type=jnp.float32,
    )
    active = jax.nn.gelu(hidden, approximate=True).astype(jnp.bfloat16)
    partial_out = contract_last(active, lax.all_gather(down_weight, "sp", axis=0, tiled=True))
    summed = lax.psum_scatter(
        partial_out.astype(jnp.bfloat16), "tp", scatter_dimension=1, tiled=True
    ).astype(jnp.float32)
    result = (mixed_rows + modulation[3] * summed).astype(jnp.bfloat16)
    return result.reshape(batches, rows_block, local_width)


def solution(mesh):
    in_specs = (
        P("groups", ("sp", "tp"), None),
        P("groups", ("sp", "tp"), None),
        P("groups", ("sp", "tp"), None),
        P("groups", "sp", "tp"),
        P(None, "tp"),
        P("tp", "sp"),
        P("sp", "tp"),
        P("sp", "tp"),
    )
    out_specs = P("groups", "sp", "tp")
    return jax.shard_map(body, mesh=mesh, in_specs=in_specs, out_specs=out_specs, check_vma=False)
```

profile of v0, /device:TPU:16, one launch (start us, length us, event | category | flops | bytes accessed | tf_op | source)
XLA Modules:
  0.0 484.6 jit_solution(9389380854067668467)
XLA Ops:
  6.5 0.0 copy-start
  6.5 0.0 copy-start.1
  6.5 0.0 all-gather.4.cloned.1.call-start
  6.5 0.7 all-gather.4.cloned.1.call-update
  7.3 0.0 all-gather.6.cloned.1.call-start
  7.3 0.7 all-gather.6.cloned.1.call-update
  8.0 0.0 all-gather.8.cloned.1.call-start
  8.1 0.7 all-gather.8.cloned.1.call-update
  8.7 0.0 copy-done
  8.8 0.0 copy-start.2
  8.8 2.8 copy.32
  11.6 2.8 reshape.53
  14.4 5.2 %all-to-all-start = ((bf16[4,2,8192]{2,1,0:T(2,128)(2,1)}), bf16[4,2,8192]{2,1,0:T(2,128)(2,1)S(1)}, u32[]{:S(2)}, u32[]{:S(2)}) async-start(bf16[4,2,8192]{2,1,0:T(2,128)(2,1)} %reshape.53), calls=%async_computation | async-start | bytes 262144 | tf_op jit(solution)/shard_map/all_to_all | solution.py:21
  19.6 0.0 copy-done.1
  19.6 2.7 copy.36
  22.3 2.8 reshape.55
  25.2 2.2 all-to-all-done
  27.4 6.6 %all-to-all-start.1 = ((bf16[4,2,8192]{2,1,0:T(2,128)(2,1)}), bf16[4,2,8192]{2,1,0:T(2,128)(2,1)S(1)}, u32[]{:S(2)}, u32[]{:S(2)}) async-start(bf16[4,2,8192]{2,1,0:T(2,128)(2,1)} %reshape.55), calls=%async_computation.1 | async-start | bytes 262144 | tf_op jit(solution)/shard_map/all_to_all | solution.py:20
  34.0 0.0 copy-done.2
  34.0 2.7 copy.40
  36.7 2.8 reshape.51
  39.5 2.4 reshape.54
  42.0 1.3 copy.50
  43.4 0.0 all-to-all-done.1
  43.4 5.1 %all-to-all-start.2 = ((bf16[4,2,8192]{2,1,0:T(2,128)(2,1)}), bf16[4,2,8192]{2,1,0:T(2,128)(2,1)S(1)}, u32[]{:S(2)}, u32[]{:S(2)}) async-start(bf16[4,2,8192]{2,1,0:T(2,128)(2,1)} %reshape.51), calls=%async_computation.2 | async-start | bytes 262144 | tf_op jit(solution)/shard_map/all_to_all | solution.py:22
  48.5 7.1 %all_gather.21 = bf16[2,128,1024]{2,1,0:T(8,128)(2,1)S(1)} all-gather(bf16[2,32,1024]{2,1,0:T(8,128)(2,1)S(1)} %bitcast.66), channel_id=1, replica_groups=mesh['groups'=2,'tp'=4,'sp'=4] {'tp'}, dimensions={1}, use_global_device_ids=true | all-gather | bytes 655360 | tf_op jit(solution)/shard_map/all_gather | solution.py:76
  55.7 0.3 copy.35
  55.9 2.5 reshape.56
  58.4 1.2 copy.37
  59.6 0.0 copy-start.4
  59.7 0.0 copy-start.3
  59.7 0.0 all-to-all-done.2
  59.7 2.5 reshape.52
  62.1 1.3 copy.51
  63.6 7.3 %all_gather.22 = bf16[2,128,1024]{2,1,0:T(8,128)(2,1)S(1)} all-gather(bf16[2,32,1024]{2,1,0:T(8,128)(2,1)S(1)} %bitcast.70), channel_id=1, replica_groups=mesh['groups'=2,'tp'=4,'sp'=4] {'tp'}, dimensions={1}, use_global_device_ids=true | all-gather | bytes 655360 | tf_op jit(solution)/shard_map/all_gather | solution.py:77
  70.8 0.3 copy.43
  71.1 0.3 fusion.29
  71.4 0.3 fusion.13
  71.7 0.4 fusion.3
  72.2 0.1 copy.52
  72.2 0.7 reshape.44
  72.9 5.1 %all-to-all-start.3 = ((bf16[2,32,1024]{2,0,1:T(2,128)(2,1)}), bf16[2,32,1024]{2,0,1:T(2,128)(2,1)S(1)}, u32[]{:S(2)}, u32[]{:S(2)}) async-start(bf16[2,32,1024]{2,0,1:T(2,128)(2,1)} %reshape.44), calls=%async_computation.3 | async-start | bytes 262144 | tf_op jit(solution)/shard_map/all_to_all | solution.py:82
  78.0 0.0 reduce-scatter.4.cloned.1.call-start
  78.0 0.0 copy-done.4
  78.1 6.0 %all-to-all-done.3 = bf16[2,32,1024]{2,0,1:T(2,128)(2,1)S(1)} async-done(((bf16[2,32,1024]{2,0,1:T(2,128)(2,1)}), bf16[2,32,1024]{2,0,1:T(2,128)(2,1)S(1)}, u32[]{:S(2)}, u32[]{:S(2)}) %all-to-all-start.3) | async-done | bytes 131104 | tf_op jit(solution)/shard_map/all_to_all | solution.py:82
  84.0 0.1 copy.64
  84.1 0.1 all_to_all.64
  84.2 7.0 %all_gather.23 = bf16[2,32,4096]{2,1,0:T(8,128)(2,1)S(1)} all-gather(bf16[2,8,4096]{2,1,0:T(8,128)(2,1)S(1)} %all_to_all.64), channel_id=1, replica_groups=mesh['groups'=2,'tp'=4,'sp'=4] {'tp'}, dimensions={1}, use_global_device_ids=true | all-gather | bytes 655360 | tf_op jit(solution)/shard_map/all_gather | solution.py:89
  91.2 24.1 %all-gather.4.cloned.1.call-done = bf16[640,4096]{1,0:T(8,128)(2,1)} async-done(((bf16[640,1024]{1,0:T(8,128)(2,1)}), bf16[640,4096]{1,0:T(8,128)(2,1)}) %all-gather.4.cloned.1.call-update) | async-done | bytes 5242896 | tf_op jit(solution)/shard_map/all_gather | solution.py:95
  115.4 0.0 copy-done.3
  115.4 4.3 fusion.28
  119.7 6.9 %all-reduce = (f32[64]{0:T(128)S(1)}, f32[64]{0:T(128)S(1)}) all-reduce(f32[64]{0:T(128)S(1)} %get-tuple-element.6, f32[64]{0:T(128)S(1)} %get-tuple-element.5), channel_id=1, replica_groups=mesh['groups'=2,'tp'=4,'sp'=4] {'tp'}, use_global_device_ids=true, to_apply=%region_5.0 | all-reduce | flops 128 | bytes 1024 | tf_op jit(solution)/shard_map/psum | solution.py:99
  126.6 0.1 add_convert_fusion.1
  126.7 6.1 %all_gather.25 = bf16[64,2560]{1,0:T(8,128)(2,1)S(1)} all-gather(bf16[64,640]{1,0:T(8,128)(2,1)S(1)} %add_convert_fusion.1), channel_id=1, replica_groups=mesh['groups'=2,'tp'=4,'sp'=4] {'tp'}, dimensions={1}, use_global_device_ids=true | all-gather | bytes 409600 | tf_op jit(solution)/shard_map/all_gather | solution.py:110
  132.8 146.9 %all-gather.6.cloned.1.call-done = bf16[2560,1792]{1,0:T(8,128)(2,1)} async-done(((bf16[640,1792]{1,0:T(8,128)(2,1)}), bf16[2560,1792]{1,0:T(8,128)(2,1)}) %all-gather.6.cloned.1.call-update) | async-done | bytes 9175056 | tf_op jit(solution)/shard_map/all_gather | solution.py:114
  279.8 162.3 %all-gather.8.cloned.1.call-done = bf16[2560,1792]{1,0:T(8,128)(2,1)} async-done(((bf16[640,1792]{1,0:T(8,128)(2,1)}), bf16[2560,1792]{1,0:T(8,128)(2,1)}) %all-gather.8.cloned.1.call-update) | async-done | bytes 9175056 | tf_op jit(solution)/shard_map/all_gather | solution.py:118
  442.0 10.7 %convolution_convert_fusion = bf16[64,2560]{1,0:T(8,128)(2,1)S(1)} fusion(bf16[2560,1792]{1,0:T(8,128)(2,1)} %all-gather.8.cloned.1.call-done, bf16[64,2560]{1,0:T(8,128)(2,1)S(1)} %all_gather.25, bf16[2560,1792]{1,0:T(8,128)(2,1)} %all-gather.6.cloned.1.call-done), kind=kOutput, calls=%fused_computation | convolution fusion | flops 1175601152 | bytes 19005440 | tf_op jit(solution)/shard_map/dot_general | solution.py:13
  452.7 1.1 copy.53
  453.8 0.0 reduce-scatter.4.cloned.1.call-update
  453.8 22.6 %reduce-scatter.4.cloned.1.call-done = bf16[640,64]{1,0:T(8,128)(2,1)} async-done(((bf16[2560,64]{1,0:T(8,128)(2,1)}), bf16[640,64]{1,0:T(8,128)(2,1)}) %reduce-scatter.4.cloned.1.call-update) | async-done | bytes 81936
  476.4 1.0 copy.54
  477.4 0.7 add_convert_fusion
  (6 shorter events, 0.2 us)
Async XLA Ops:
  6.5 2.2 copy-start
  6.5 13.0 %copy-start.1 = (bf16[2,8,4096]{2,1,0:T(8,128)(2,1)S(1)}, bf16[2,8,4096]{2,1,0:T(8,128)(2,1)}, u32[]{:S(2)}) copy-start(bf16[2,8,4096]{2,1,0:T(8,128)(2,1)} %param.8) | copy-start | bytes 393220
  6.5 108.8 %all-gather.4.cloned.1.call-start = ((), (), s32[]{:S(2)}) async-start(), calls=%async_computation.5 | async-start | bytes 6553600 | tf_op jit(solution)/shard_map/all_gather | solution.py:95
  7.3 272.5 %all-gather.6.cloned.1.call-start = ((), (), s32[]{:S(2)}) async-start(), calls=%async_computation.6 | async-start | bytes 11468800 | tf_op jit(solution)/shard_map/all_gather | solution.py:114
  8.0 434.0 %all-gather.8.cloned.1.call-start = ((), (), s32[]{:S(2)}) async-start(), calls=%async_computation.7 | async-start | bytes 11468800 | tf_op jit(solution)/shard_map/all_gather | solution.py:118
  8.8 25.2 %copy-start.2 = (bf16[2,8,4096]{2,1,0:T(8,128)(2,1)S(1)}, bf16[2,8,4096]{2,1,0:T(8,128)(2,1)}, u32[]{:S(2)}) copy-start(bf16[2,8,4096]{2,1,0:T(8,128)(2,1)} %param.10) | copy-start | bytes 393220
  14.4 13.0 %all-to-all-start = ((bf16[4,2,8192]{2,1,0:T(2,128)(2,1)}), bf16[4,2,8192]{2,1,0:T(2,128)(2,1)S(1)}, u32[]{:S(2)}, u32[]{:S(2)}) async-start(bf16[4,2,8192]{2,1,0:T(2,128)(2,1)} %reshape.53), calls=%async_computation | async-start | bytes 262144 | tf_op jit(solution)/shard_map/all_to_all | solution.py:21
  27.4 16.0 %all-to-all-start.1 = ((bf16[4,2,8192]{2,1,0:T(2,128)(2,1)}), bf16[4,2,8192]{2,1,0:T(2,128)(2,1)S(1)}, u32[]{:S(2)}, u32[]{:S(2)}) async-start(bf16[4,2,8192]{2,1,0:T(2,128)(2,1)} %reshape.55), calls=%async_computation.1 | async-start | bytes 262144 | tf_op jit(solution)/shard_map/all_to_all | solution.py:20
  43.4 16.3 %all-to-all-start.2 = ((bf16[4,2,8192]{2,1,0:T(2,128)(2,1)}), bf16[4,2,8192]{2,1,0:T(2,128)(2,1)S(1)}, u32[]{:S(2)}, u32[]{:S(2)}) async-start(bf16[4,2,8192]{2,1,0:T(2,128)(2,1)} %reshape.51), calls=%async_computation.2 | async-start | bytes 262144 | tf_op jit(solution)/shard_map/all_to_all | solution.py:22
  59.6 18.4 %copy-start.4 = (f32[4,640]{1,0:T(4,128)S(1)}, f32[4,640]{1,0:T(4,128)}, u32[]{:S(2)}) copy-start(f32[4,640]{1,0:T(4,128)} %param.12) | copy-start | bytes 30724
  59.7 55.7 %copy-start.3 = (bf16[2,32,640]{2,1,0:T(8,128)(2,1)S(1)}, bf16[2,32,640]{2,1,0:T(8,128)(2,1)}, u32[]{:S(2)}) copy-start(bf16[2,32,640]{2,1,0:T(8,128)(2,1)} %param.11) | copy-start | bytes 245764
  72.9 11.1 %all-to-all-start.3 = ((bf16[2,32,1024]{2,0,1:T(2,128)(2,1)}), bf16[2,32,1024]{2,0,1:T(2,128)(2,1)S(1)}, u32[]{:S(2)}, u32[]{:S(2)}) async-start(bf16[2,32,1024]{2,0,1:T(2,128)(2,1)} %reshape.44), calls=%async_computation.3 | async-start | bytes 262144 | tf_op jit(solution)/shard_map/all_to_all | solution.py:82
  78.0 398.4 %reduce-scatter.4.cloned.1.call-start = ((), (), s32[]{:S(2)}) async-start(), calls=%async_computation.8 | async-start | bytes 819200
Sparse Core Ops, SparseCore 0:
  8.9 106.4 all-gather.3
  116.9 162.7 all-gather.5
  281.3 160.6 all-gather.7
  453.9 22.3 reduce-scatter.3
where the time goes:
time: 487 us; the launch traced here: 485 us
  waiting for transfers between devices  366 us (75%)
  blocking collectives  34.5 us (7%)
  local copies, waits for them, and re-layouts  31.7 us (7%)
  starting transfers between devices  22.1 us (5%)
  matrix products  15.7 us (3%)
  between operations  13.3 us (3%)
    all_gather x1, waiting for transfers between devices, body(): lax.all_gather(down_weight, 'sp', axis=0, tiled=True)  162 us
    all_gather x1, waiting for transfers between devices, body(): lax.all_gather(up_weight, 'sp', axis=0, tiled=True)  147 us
    unnamed x22, local copies, waits for them, and re-layouts  26.3 us
    unnamed x5, waiting for transfers between devices  24.7 us
    all_gather x1, waiting for transfers between devices, body(): lax.all_gather(out_weight, 'sp', axis=1, tiled=True)  24.1 us
    dot_general x2, matrix products, contract_last(): lax.dot_general(left, right, (((1,), (1,)), ((), ())), preferred_element_...  15 us
  transfers between devices with their start and end apart: 8, of which 6 were waited for; matrix products, arithmetic and copies ran while one was open for 7% of the time, Pallas kernels for 0%

commit v1 on v0

--- a/solution.py
+++ b/solution.py
@@ -123,6 +123,63 @@
     return result.reshape(batches, rows_block, local_width)
 
 
+def stationary(
+    query_rows, key_rows, value_rows, residual, modulation, out_weight, up_weight, down_weight
+):
+    both = ("sp", "tp")
+    stacked = jnp.stack((query_rows, key_rows, value_rows))
+    mine = lax.all_to_all(stacked, both, split_axis=3, concat_axis=2, tiled=True)
+    batches, tokens, width = mine.shape[1:]
+    local_heads = width // HEAD_FEATURES
+    heads = mine.reshape(3, batches, tokens, local_heads, HEAD_FEATURES)
+    scores = jnp.einsum(
+        "bqhd,bkhd->bhqk", heads[0], heads[1], preferred_element_type=jnp.float32
+    ) * (1.0 / math.sqrt(HEAD_FEATURES))
+    exponent = jnp.exp(scores - jnp.max(scores, axis=-1, keepdims=True))
+    row_total = jnp.sum(exponent, axis=-1)
+    weighted = jnp.einsum(
+        "bhqk,bkhd->bqhd",
+        exponent.astype(jnp.bfloat16),
+        heads[2],
+        preferred_element_type=jnp.float32,
+    )
+    attended = (weighted / jnp.swapaxes(row_total, 1, 2)[..., None]).astype(jnp.bfloat16)
+    attended = attended.reshape(batches, tokens, width)
+    attended = lax.all_gather(attended, "tp", axis=2, tiled=True)
+    row_count = batches * tokens
+    partial = contract_last(attended.reshape(row_count, -1), out_weight)
+    partial = partial.astype(jnp.bfloat16).reshape(batches, tokens, -1)
+    projected = lax.psum_scatter(partial, "sp", scatter_dimension=1, tiled=True)
+    mixed = residual.astype(jnp.float32) + modulation[0] * projected.astype(jnp.float32)
+    first_sum, second_sum = lax.psum(
+        (jnp.sum(mixed, axis=2), jnp.sum(mixed * mixed, axis=2)), "tp"
+    )
+    row_mean = first_sum / D
+    spread = second_sum / D - row_mean * row_mean
+    normed = (
+        (mixed - row_mean[..., None])
+        * lax.rsqrt(spread[..., None] + 1e-06)
+        * (1.0 + modulation[2])
+        + modulation[1]
+    ).astype(jnp.bfloat16)
+    normed = lax.all_gather(normed, "tp", axis=2, tiled=True)
+    normed = lax.all_to_all(normed, "sp", split_axis=2, concat_axis=1, tiled=True)
+    hidden = jnp.dot(
+        normed.reshape(row_count, -1), up_weight, preferred_element_type=jnp.float32
+    )
+    hidden = hidden.astype(jnp.bfloat16).reshape(batches, tokens, -1)
+    hidden = lax.psum_scatter(hidden, "sp", scatter_dimension=1, tiled=True)
+    active = jax.nn.gelu(hidden.astype(jnp.float32), approximate=True).astype(jnp.bfloat16)
+    active = lax.all_gather(active, "sp", axis=1, tiled=True)
+    down = contract_last(active.reshape(row_count, -1), down_weight)
+    down = down.astype(jnp.bfloat16).reshape(batches, tokens, -1)
+    down = lax.psum_scatter(down, "tp", scatter_dimension=1, tiled=True)
+    size = lax.axis_size("tp")
+    swap = [(s * size + t, t * size + s) for s in range(size) for t in range(size)]
+    down = lax.ppermute(down, ("tp", "sp"), swap)
+    return (mixed + modulation[3] * down.astype(jnp.float32)).astype(jnp.bfloat16)
+
+
 def solution(mesh):
     in_specs = (
         P("groups", ("sp", "tp"), None),
@@ -135,4 +192,12 @@
         P("sp", "tp"),
     )
     out_specs = P("groups", "sp", "tp")
-    return jax.shard_map(body, mesh=mesh, in_specs=in_specs, out_specs=out_specs, check_vma=False)
+    def block(*operands):
+        sizes = mesh.shape
+        rows = operands[0].shape[0] * operands[0].shape[1] * sizes["sp"] * sizes["tp"]
+        square = sizes["sp"] == sizes["tp"]
+        whole_heads = operands[0].shape[2] % (sizes["sp"] * sizes["tp"] * HEAD_FEATURES) == 0
+        few = rows < operands[6].shape[0]
+        return (stationary if square and whole_heads and few else body)(*operands)
+
+    return jax.shard_map(block, mesh=mesh, in_specs=in_specs, out_specs=out_specs, check_vma=False)

time: 487 us -> 261 us (0.54)
  waiting for transfers between devices: 366 us -> 99.7 us
  local copies, waits for them, and re-layouts: 31.7 us -> 66.7 us
  blocking collectives: 34.5 us -> 66.8 us
  starting transfers between devices: 22.1 us -> 2.01 us
  matrix products: 15.7 us -> 6.77 us
    all_gather x3 -> x0, waiting for transfers between devices: 333 us -> none  [the longest x1 162 us: body(): lax.all_gather(down_weight, 'sp', axis=0, tiled=True)]
    unnamed x5, waiting for transfers between devices: 24.7 us -> 68.1 us
    all_to_all x0 -> x2, blocking collectives: none -> 29.4 us  [the longest x1 17 us: stationary(): lax.all_to_all(stacked, both, split_axis=3, concat_axis=2, tiled=True)]
    reduce_scatter x0 -> x1, waiting for transfers between devices: none -> 24.8 us  [stationary(): hidden = lax.psum_scatter(hidden, 'sp', scatter_dimension=1, tiled=True)]
    all_to_all x4 -> x0, starting transfers between devices: 22 us -> none  [the longest x1 6.6 us: attend(): lax.all_to_all(query_part, 'sp', split_axis=2, concat_axis=1, tiled=True)]
    all_to_all x7 -> x3, local copies, waits for them, and re-layouts: 4.2 us -> 16.8 us  [the longest x1 13.3 us: stationary(): lax.all_to_all(stacked, both, split_axis=3, concat_axis=2, tiled=True)]
    another operation x0 -> x1, local copies, waits for them, and re-layouts: none -> 10.7 us  [stationary(): stacked = jnp.stack((query_rows, key_rows, value_rows))]
    dot_general x2, matrix products: 15 us -> 4.5 us  [contract_last(): lax.dot_general(left, right, (((1,), (1,)), ((), ())), preferred_element_...]
  transfers between devices with their start and end apart: 8 -> 4, of which waited for: 6 -> 4; matrix products, arithmetic and copies ran while one was open for 7% -> 0% of each run, Pallas kernels for 0% -> 0%
where the time goes in v1:
time: 261 us; the launch traced here: 260 us
  waiting for transfers between devices  99.7 us (38%)
  blocking collectives  66.8 us (26%)
  local copies, waits for them, and re-layouts  66.7 us (26%)
  between operations  14.6 us (6%)
  matrix products  6.77 us (3%)
  other arithmetic  3.33 us (1%)
    unnamed x5, waiting for transfers between devices  68.1 us
    unnamed x18, local copies, waits for them, and re-layouts  34.6 us
    reduce_scatter x1, waiting for transfers between devices, stationary(): hidden = lax.psum_scatter(hidden, 'sp', scatter_dimension=1, tiled=True)  24.8 us
    all_gather x1, blocking collectives, stationary(): active = lax.all_gather(active, 'sp', axis=1, tiled=True)  18.9 us
    all_to_all x1, blocking collectives, stationary(): lax.all_to_all(stacked, both, split_axis=3, concat_axis=2, tiled=True)  17 us
    all_to_all x1, local copies, waits for them, and re-layouts, stationary(): lax.all_to_all(stacked, both, split_axis=3, concat_axis=2, tiled=True)  13.3 us
    all_to_all x1, blocking collectives, stationary(): lax.all_to_all(normed, 'sp', split_axis=2, concat_axis=1, tiled=True)  12.3 us
    another operation x1, local copies, waits for them, and re-layouts, stationary(): stacked = jnp.stack((query_rows, key_rows, value_rows))  10.7 us
  transfers between devices with their start and end apart: 4, of which 4 were waited for; matrix products, arithmetic and copies ran while one was open for 0% of the time, Pallas kernels for 0%

profile of v1, /device:TPU:16, one launch (start us, length us, event | category | flops | bytes accessed | tf_op | source)
XLA Modules:
  0.0 259.9 jit_solution(14532735664056187032)
XLA Ops:
  6.5 0.0 copy-start
  6.5 0.0 all-reduce.6.cloned.1.call-start
  6.5 1.2 pad_maximum_fusion
  7.8 10.7 %copy.54 = bf16[3,2,8,4096]{2,1,0,3:T(2,128)(2,1)} copy(bf16[3,2,8,4096]{3,2,1,0:T(8,128)(2,1)S(1)} %pad_maximum_fusion) | data formatting | bytes 786432 | tf_op jit(solution)/shard_map/stack | solution.py:130
  18.5 17.7 %reshape.59 = bf16[16,2,6144]{2,1,0:T(2,128)(2,1)S(1)} reshape(bf16[4096,3,2,8]{3,2,1,0:T(2,128)(2,1)} %bitcast.39) | data formatting | bytes 786432
  36.2 17.0 %all_to_all.30 = bf16[16,2,6144]{2,1,0:T(2,128)(2,1)S(1)} all-to-all(bf16[16,2,6144]{2,1,0:T(2,128)(2,1)S(1)} %reshape.59), channel_id=1, replica_groups=mesh['groups'=2,'tp'=4,'sp'=4] {'sp','tp'}, dimensions={0} | all-to-all | bytes 786432 | tf_op jit(solution)/shard_map/all_to_all | solution.py:131
  53.2 8.3 %reshape.60 = bf16[4096,3,2,8]{3,2,1,0:T(2,128)(2,1)} reshape(bf16[16,2,6144]{2,1,0:T(2,128)(2,1)S(1)} %all_to_all.30) | data formatting | bytes 786432
  61.6 13.3 %copy.55 = bf16[3,2,8,16,256]{4,2,3,1,0:T(8,128)(2,1)S(1)} copy(bf16[3,2,8,16,256]{2,1,0,4,3:T(2,128)(2,1)} %bitcast.40) | data formatting | bytes 786432 | tf_op jit(solution)/shard_map/all_to_all | solution.py:131
  75.0 0.2 fusion.17
  75.2 0.1 fusion.8
  75.3 0.2 fusion.1
  75.5 0.0 copy-start.4
  75.5 0.0 copy-start.2
  75.5 0.0 copy-start.1
  75.6 0.1 copy.60
  75.7 6.5 %all_gather.9 = bf16[2,128,1024]{2,1,0:T(8,128)(2,1)S(1)} all-gather(bf16[2,128,256]{2,1,0:T(8,128)(2,1)S(1)} %copy.60), channel_id=1, replica_groups=mesh['groups'=2,'tp'=4,'sp'=4] {'tp'}, dimensions={2}, use_global_device_ids=true | all-gather | bytes 655360 | tf_op jit(solution)/shard_map/all_gather | solution.py:148
  82.2 1.9 convolution_convert_fusion.2
  84.1 1.1 copy.61
  85.2 0.0 all-reduce.6.cloned.1.call-update
  85.2 0.0 reduce-scatter.2.cloned.1.call-start
  85.3 0.0 copy-done.4
  85.3 0.6 dynamic-slice
  86.5 0.0 copy-done.2
  86.5 35.1 %all-reduce.6.cloned.1.call-done = bf16[2,128,640]{2,0,1:T(2,128)(2,1)} async-done(((bf16[2,128,640]{2,0,1:T(2,128)(2,1)}), bf16[2,128,640]{2,0,1:T(2,128)(2,1)}) %all-reduce.6.cloned.1.call-update) | async-done | bytes 327696
  121.7 0.9 constant_dynamic-slice_fusion.1
  122.6 0.0 copy-done.1
  122.6 0.1 fusion.15
  122.8 5.7 %all-reduce.2 = (f32[2,32]{1,0:T(2,128)S(1)}, f32[2,32]{1,0:T(2,128)S(1)}) all-reduce(f32[2,32]{1,0:T(2,128)S(1)} %get-tuple-element.6, f32[2,32]{1,0:T(2,128)S(1)} %get-tuple-element.5), channel_id=1, replica_groups=mesh['groups'=2,'tp'=4,'sp'=4] {'tp'}, use_global_device_ids=true, to_apply=%region_6.0 | all-reduce | flops 128 | bytes 1024 | tf_op jit(solution)/shard_map/psum | solution.py:154
  128.4 0.1 add_convert_fusion.1
  128.6 6.3 %all_gather.10 = bf16[2,32,2560]{2,1,0:T(8,128)(2,1)S(1)} all-gather(bf16[2,32,640]{2,1,0:T(8,128)(2,1)S(1)} %add_convert_fusion.1), channel_id=1, replica_groups=mesh['groups'=2,'tp'=4,'sp'=4] {'tp'}, dimensions={2}, use_global_device_ids=true | all-gather | bytes 409600 | tf_op jit(solution)/shard_map/all_gather | solution.py:165
  134.9 2.2 copy.63
  137.1 3.7 %reshape.61 = bf16[4,2,20480]{2,1,0:T(2,128)(2,1)S(1)} reshape(bf16[2560,2,32]{2,1,0:T(2,128)(2,1)} %bitcast.41) | data formatting | bytes 655360
  140.8 12.3 %all_to_all.31 = bf16[4,2,20480]{2,1,0:T(2,128)(2,1)S(1)} all-to-all(bf16[4,2,20480]{2,1,0:T(2,128)(2,1)S(1)} %reshape.61), channel_id=1, replica_groups=mesh['groups'=2,'tp'=4,'sp'=4] {'sp'}, dimensions={0} | all-to-all | bytes 655360 | tf_op jit(solution)/shard_map/all_to_all | solution.py:166
  153.1 1.7 reshape.62
  154.8 3.5 %copy.69 = bf16[2,32,4,640]{3,2,1,0:T(4,128)(2,1)S(1)} copy(bf16[2,32,4,640]{1,0,3,2:T(2,128)(2,1)} %bitcast.42) | data formatting | bytes 655360 | tf_op jit(solution)/shard_map/all_to_all | solution.py:166
  158.4 0.0 copy-done
  158.4 1.8 convolution_convert_fusion
  160.2 0.0 reduce-scatter.2.cloned.1.call-update
  160.3 0.0 all-reduce.8.cloned.1.call-start
  160.3 24.8 %reduce-scatter.2.cloned.1.call-done = bf16[2,32,1792]{2,1,0:T(8,128)(2,1)} async-done(((bf16[2,128,1792]{2,1,0:T(8,128)(2,1)}), bf16[2,32,1792]{2,1,0:T(8,128)(2,1)}) %reduce-scatter.2.cloned.1.call-update) | async-done | bytes 229392 | tf_op jit(solution)/shard_map/reduce_scatter | solution.py:171
  185.1 1.1 fusion.7
  186.2 18.9 %all_gather.11 = bf16[2,128,1792]{2,1,0:T(8,128)(2,1)S(1)} all-gather(bf16[2,32,1792]{2,1,0:T(8,128)(2,1)S(1)} %fusion.7), channel_id=1, replica_groups=mesh['groups'=2,'tp'=4,'sp'=4] {'sp'}, dimensions={1}, use_global_device_ids=true | all-gather | bytes 1146880 | tf_op jit(solution)/shard_map/all_gather | solution.py:173
  205.2 0.0 copy-start.3
  205.2 2.6 convolution_convert_fusion.1
  207.8 1.1 copy.66
  208.8 0.0 all-reduce.8.cloned.1.call-update
  208.9 0.0 copy-done.3
  208.9 0.6 dynamic-slice.2
  210.1 32.9 %all-reduce.8.cloned.1.call-done = bf16[2,128,640]{2,0,1:T(2,128)(2,1)} async-done(((bf16[2,128,640]{2,0,1:T(2,128)(2,1)}), bf16[2,128,640]{2,0,1:T(2,128)(2,1)}) %all-reduce.8.cloned.1.call-update) | async-done | bytes 327696
  243.0 0.9 constant_dynamic-slice_fusion
  244.0 1.9 collective-permute-start
  245.9 6.7 %collective-permute-done = bf16[2,32,640]{2,1,0:T(8,128)(2,1)S(1)} collective-permute-done((bf16[2,32,640]{2,1,0:T(8,128)(2,1)S(1)}, bf16[2,32,640]{2,1,0:T(8,128)(2,1)S(1)}, u32[]{:S(2)}, u32[]{:S(2)}) %collective-permute-start) | collective-permute-done | bytes 81952 | tf_op jit(solution)/shard_map/ppermute | solution.py:179
  252.7 0.7 add_convert_fusion
  (8 shorter events, 0.2 us)
Async XLA Ops:
  6.5 151.9 %copy-start = (bf16[640,1792]{1,0:T(8,128)(2,1)S(1)}, bf16[640,1792]{1,0:T(8,128)(2,1)}, u32[]{:S(2)}) copy-start(bf16[640,1792]{1,0:T(8,128)(2,1)} %param.14) | copy-start | bytes 6881284
  6.5 115.2 %all-reduce.6.cloned.1.call-start = ((), (), s32[]{:S(2)}) async-start(), calls=%async_computation.4 | async-start | bytes 655360
  75.5 9.7 %copy-start.4 = (u32[32]{0:T(128)S(1)}, u32[32]{0:T(128)}, u32[]{:S(2)}) copy-start(u32[32]{0:T(128)} %constant.26) | copy-start | bytes 388
  75.5 11.0 %copy-start.2 = (f32[4,640]{1,0:T(4,128)S(1)}, f32[4,640]{1,0:T(4,128)}, u32[]{:S(2)}) copy-start(f32[4,640]{1,0:T(4,128)} %param.12) | copy-start | bytes 30724
  75.5 47.1 %copy-start.1 = (bf16[2,32,640]{2,1,0:T(8,128)(2,1)S(1)}, bf16[2,32,640]{2,1,0:T(8,128)(2,1)}, u32[]{:S(2)}) copy-start(bf16[2,32,640]{2,1,0:T(8,128)(2,1)} %param.11) | copy-start | bytes 245764
  85.2 99.9 %reduce-scatter.2.cloned.1.call-start = ((), (), s32[]{:S(2)}) async-start(), calls=%async_computation.3 | async-start | bytes 1146880 | tf_op jit(solution)/shard_map/reduce_scatter | solution.py:171
  160.3 82.8 %all-reduce.8.cloned.1.call-start = ((), (), s32[]{:S(2)}) async-start(), calls=%async_computation.5 | async-start | bytes 655360
  205.2 3.7 %copy-start.3 = (u32[32]{0:T(128)S(1)}, u32[32]{0:T(128)}, u32[]{:S(2)}) copy-start(u32[32]{0:T(128)} %constant.30) | copy-start | bytes 388
  244.0 8.7 %collective-permute-start = (bf16[2,32,640]{2,1,0:T(8,128)(2,1)S(1)}, bf16[2,32,640]{2,1,0:T(8,128)(2,1)S(1)}, u32[]{:S(2)}, u32[]{:S(2)}) collective-permute-start(bf16[2,32,640]{2,1,0:T(8,128)(2,1)S(1)} %copy.67), channel_id=1, source_target_pairs={{0,0},{1,4},{2,8},{3,12},{4,1},{5,5},{6,9},{7,13},{8,2},{9,6},{10,... | collective-permute-start | bytes 245768 | tf_op jit(solution)/shard_map/ppermute | solution.py:179
Sparse Core Ops, SparseCore 0:
  85.3 36.3 all-reduce.5
  160.4 24.7 reduce-scatter.1
  209.0 34.0 all-reduce.7

commit v2 on v0

--- a/solution.py
+++ b/solution.py
@@ -1,12 +1,16 @@
+import functools
 import math
 
 import jax
 import jax.numpy as jnp
 from jax import lax
+from jax.experimental import pallas as pl
+from jax.experimental.pallas import tpu as pltpu
 from jax.sharding import PartitionSpec as P
 
 D = 2560
 HEAD_FEATURES = 128
+BAND = 256
 
 
 def contract_last(left, right):
@@ -123,6 +127,492 @@
     return result.reshape(batches, rows_block, local_width)
 
 
+def block_kernel(
+    ranks,
+    stages,
+    chunks,
+    query_ref,
+    key_ref,
+    value_ref,
+    residual_ref,
+    modulation_ref,
+    out_hbm,
+    up_hbm,
+    down_hbm,
+    result_ref,
+    out_weight,
+    up_weight,
+    down_weight,
+    heads,
+    attended,
+    projected,
+    outgoing,
+    incoming,
+    mixed,
+    sums,
+    normed_out,
+    normed,
+    hidden_out,
+    hidden_in,
+    active,
+    down_total,
+    down_out,
+    down_in,
+    last_out,
+    last_in,
+    out_sem,
+    weight_sem,
+    own_sem,
+    head_send,
+    head_recv,
+    attend_send,
+    attend_recv,
+    project_send,
+    project_recv,
+    sums_send,
+    sums_recv,
+    normed_send,
+    normed_recv,
+    hidden_send,
+    hidden_recv,
+    active_send,
+    active_recv,
+    down_send,
+    down_recv,
+    last_send,
+    last_recv,
+):
+    t, s = lax.axis_index("tp"), lax.axis_index("sp")
+    members = ranks * stages
+    me = s * ranks + t
+    batches, few_tokens, _ = query_ref.shape
+    width = heads.shape[-1]
+    tokens = members * few_tokens
+    part = tokens // stages
+    rows = batches * part
+    half = rows * stages // 2
+    band = hidden_in.shape[-1]
+
+    def remote(source, target, send, recv, rank, stage):
+        return pltpu.make_async_remote_copy(
+            src_ref=source,
+            dst_ref=target,
+            send_sem=send,
+            recv_sem=recv,
+            device_id={"tp": rank, "sp": stage},
+            device_id_type=pl.DeviceIdType.MESH,
+        )
+
+    out_copy = pltpu.make_async_copy(out_hbm, out_weight, out_sem)
+    up_copies, down_copies_in = (
+        [
+            pltpu.make_async_copy(
+                source.at[:, chunk * band : (chunk + 1) * band],
+                target.at[chunk],
+                weight_sem.at[at, chunk],
+            )
+            for chunk in range(chunks)
+        ]
+        for at, (source, target) in enumerate(((up_hbm, up_weight), (down_hbm, down_weight)))
+    )
+    for copy in [out_copy, *up_copies, *down_copies_in]:
+        copy.start()
+
+    barrier = pltpu.get_barrier_semaphore()
+    for offset in range(1, members):
+        other = lax.rem(me + offset, members)
+        pl.semaphore_signal(
+            barrier,
+            inc=1,
+            device_id={"tp": lax.rem(other, ranks), "sp": lax.div(other, ranks)},
+            device_id_type=pl.DeviceIdType.MESH,
+        )
+    pl.semaphore_wait(barrier, members - 1)
+
+    def head_copy(at, source, offset):
+        other = lax.rem(me + offset, members)
+        columns = pl.ds(pl.multiple_of(other * width, width), width)
+        return remote(
+            source.at[:, :, columns],
+            heads.at[at, me],
+            head_send.at[at, offset - 1],
+            head_recv.at[at, offset - 1],
+            lax.rem(other, ranks),
+            lax.div(other, ranks),
+        )
+
+    sources = (query_ref, key_ref, value_ref)
+    head_copies = [
+        head_copy(at, source, offset)
+        for offset in range(1, members)
+        for at, source in enumerate(sources)
+    ]
+    for copy in head_copies:
+        copy.start()
+    own_columns = pl.ds(pl.multiple_of(me * width, width), width)
+    own_copies = [
+        pltpu.make_async_copy(source.at[:, :, own_columns], heads.at[at, me], own_sem.at[at])
+        for at, source in enumerate(sources)
+    ]
+    for copy in own_copies:
+        copy.start()
+    for copy in own_copies:
+        copy.wait()
+    for copy in head_copies:
+        copy.wait_recv()
+
+    def head_rows(at, batch, columns):
+        loaded = heads[at, :, batch, :, columns].astype(jnp.float32)
+        return loaded.reshape(tokens, HEAD_FEATURES).astype(jnp.bfloat16)
+
+    score_scale = 1.0 / math.sqrt(HEAD_FEATURES)
+    attend_copies = []
+    for batch in range(batches):
+        for head in range(width // HEAD_FEATURES):
+            columns = slice(head * HEAD_FEATURES, (head + 1) * HEAD_FEATURES)
+            scores = score_scale * contract_last(
+                head_rows(0, batch, columns), head_rows(1, batch, columns)
+            )
+            exponent = jnp.exp(scores - jnp.max(scores, axis=-1, keepdims=True))
+            row_total = jnp.sum(exponent, axis=-1, keepdims=True)
+            weighted = jnp.dot(
+                exponent.astype(jnp.bfloat16),
+                head_rows(2, batch, columns),
+                preferred_element_type=jnp.float32,
+            )
+            attended[t, batch, :, columns] = (weighted / row_total).astype(jnp.bfloat16)
+        for offset in range(1, ranks):
+            copy = remote(
+                attended.at[t, batch],
+                attended.at[t, batch],
+                attend_send.at[batch, offset - 1],
+                attend_recv.at[batch, offset - 1],
+                lax.rem(t + offset, ranks),
+                s,
+            )
+            copy.start()
+            attend_copies.append(copy)
+
+    out_copy.wait()
+    for copy in attend_copies:
+        copy.wait_recv()
+    total = None
+    for rank in range(ranks):
+        left = attended[rank].reshape(batches * tokens, width)
+        product = contract_last(left, out_weight[:, rank * width : (rank + 1) * width])
+        total = product if total is None else total + product
+    projected[...] = total.reshape(projected.shape)
+
+    project_copies = []
+    for offset in range(1, stages):
+        stage = lax.rem(s + offset, stages)
+        block = projected[:, pl.ds(pl.multiple_of(stage * part, part), part), :]
+        outgoing[offset - 1] = block.reshape(rows, -1).astype(jnp.bfloat16)
+        copy = remote(
+            outgoing.at[offset - 1],
+            incoming.at[offset - 1],
+            project_send.at[offset - 1],
+            project_recv.at[offset - 1],
+            t,
+            stage,
+        )
+        copy.start()
+        project_copies.append(copy)
+    kept = projected[:, pl.ds(pl.multiple_of(s * part, part), part), :].reshape(rows, -1)
+    for offset in range(1, stages):
+        project_copies[offset - 1].wait_recv()
+        kept = kept + incoming[offset - 1].astype(jnp.float32)
+    stream = residual_ref[...].astype(jnp.float32).reshape(rows, -1)
+    stream = stream + modulation_ref[0:1, :] * kept
+    mixed[...] = stream
+    first = jnp.sum(stream, axis=1, keepdims=True)
+    second = jnp.sum(stream * stream, axis=1, keepdims=True)
+    lanes = lax.broadcasted_iota(jnp.int32, (rows, 128), 1)
+    sums[t] = jnp.where(lanes == 0, first, second)
+    sums_copies = []
+    for offset in range(1, ranks):
+        copy = remote(
+            sums.at[t],
+            sums.at[t],
+            sums_send.at[offset - 1],
+            sums_recv.at[offset - 1],
+            lax.rem(t + offset, ranks),
+            s,
+        )
+        copy.start()
+        sums_copies.append(copy)
+    for copy in sums_copies:
+        copy.wait_recv()
+    both_sums = sums[0]
+    for rank in range(1, ranks):
+        both_sums = both_sums + sums[rank]
+    row_mean = both_sums[:, 0:1] / D
+    spread = both_sums[:, 1:2] / D - row_mean * row_mean
+    normed_rows = (
+        (mixed[...] - row_mean)
+        * lax.rsqrt(spread + 1e-06)
+        * (1.0 + modulation_ref[2:3, :])
+        + modulation_ref[1:2, :]
+    ).astype(jnp.bfloat16)
+    normed_out[...] = normed_rows
+
+    own_rows = pl.ds(pl.multiple_of(s * rows, rows), rows)
+
+    def normed_copy(offset):
+        return remote(
+            normed_out,
+            normed.at[own_rows],
+            normed_send.at[offset],
+            normed_recv.at[s],
+            lax.rem(t + offset, ranks),
+            t,
+        )
+
+    for offset in range(1, ranks):
+        normed_copy(offset).start()
+
+    @pl.when(s != t)
+    def _():
+        normed_copy(0).start()
+
+    @pl.when(s == t)
+    def _():
+        normed[own_rows, :] = normed_rows
+
+    for copy in up_copies:
+        copy.wait()
+    for stage in range(stages):
+
+        @pl.when(jnp.logical_or(t != s, s != stage))
+        def _():
+            remote(
+                normed_out,
+                normed.at[pl.ds(stage * rows, rows)],
+                normed_send.at[0],
+                normed_recv.at[stage],
+                t,
+                s,
+            ).wait_recv()
+
+    for copy in down_copies_in:
+        copy.wait()
+    down_total[...] = jnp.zeros_like(down_total)
+
+    def absorb(way, chunk):
+        block = contract_last(active[way, chunk], down_weight[chunk])
+        down_total[way * half : (way + 1) * half, :] += block
+
+    def slot(at, carry):
+        for way in range(2):
+            place = s if way == 0 else stages - 1 - s
+            toward = -1 if way == 0 else 1
+            chunk = at - (stages - 1 - place)
+
+            @pl.when(jnp.logical_and(chunk >= 0, chunk < chunks))
+            def _():
+                partial = jnp.dot(
+                    normed[way * half : (way + 1) * half, :],
+                    up_weight[chunk],
+                    preferred_element_type=jnp.float32,
+                )
+                hidden_out[way, chunk] = partial.astype(jnp.bfloat16)
+
+                def hidden_copy():
+                    return remote(
+                        hidden_out.at[way, chunk],
+                        hidden_in.at[way, chunk],
+                        hidden_send.at[way, chunk],
+                        hidden_recv.at[way, chunk],
+                        t,
+                        s + toward,
+                    )
+
+                @pl.when(place == stages - 1)
+                def _():
+                    hidden_copy().start()
+
+                @pl.when(place < stages - 1)
+                def _():
+                    hidden_copy().wait_recv()
+                    combined = partial + hidden_in[way, chunk].astype(jnp.float32)
+
+                    @pl.when(place > 0)
+                    def _():
+                        hidden_out[way, chunk] = combined.astype(jnp.bfloat16)
+                        hidden_copy().start()
+
+                    @pl.when(place == 0)
+                    def _():
+                        active[way, chunk] = jax.nn.gelu(combined, approximate=True).astype(
+                            jnp.bfloat16
+                        )
+                        active_copy(way, chunk).start()
+                        absorb(way, chunk)
+
+            back = at - (stages - 1) - place
+
+            @pl.when(jnp.logical_and(place > 0, jnp.logical_and(back >= 0, back < chunks)))
+            def _():
+                active_copy(way, back).wait_recv()
+
+                @pl.when(place < stages - 1)
+                def _():
+                    active_copy(way, back).start()
+
+                absorb(way, back)
+
+        return carry
+
+    def active_copy(way, chunk):
+        return remote(
+            active.at[way, chunk],
+            active.at[way, chunk],
+            active_send.at[way, chunk],
+            active_recv.at[way, chunk],
+            t,
+            s + (1 if way == 0 else -1),
+        )
+
+    lax.fori_loop(0, chunks + 2 * (stages - 1), slot, 0)
+
+    down_copies = []
+    for offset in range(1, ranks):
+        rank = lax.rem(t + offset, ranks)
+        block = down_total[pl.ds(pl.multiple_of(rank * rows, rows), rows), :]
+        down_out[offset - 1] = block.astype(jnp.bfloat16)
+        copy = remote(
+            down_out.at[offset - 1],
+            down_in.at[offset - 1],
+            down_send.at[offset - 1],
+            down_recv.at[offset - 1],
+            rank,
+            s,
+        )
+        copy.start()
+        down_copies.append(copy)
+    summed = down_total[pl.ds(pl.multiple_of(t * rows, rows), rows), :]
+    for offset in range(1, ranks):
+        down_copies[offset - 1].wait_recv()
+        summed = summed + down_in[offset - 1].astype(jnp.float32)
+    last_out[...] = summed.astype(jnp.bfloat16)
+    last_copy = remote(last_out, last_in, last_send, last_recv, s, t)
+
+    @pl.when(s != t)
+    def _():
+        last_copy.start()
+        last_copy.wait_recv()
+
+    @pl.when(s == t)
+    def _():
+        last_in[...] = last_out[...]
+
+    result = mixed[...] + modulation_ref[3:4, :] * last_in[...].astype(jnp.float32)
+    result_ref[...] = result.astype(jnp.bfloat16).reshape(result_ref.shape)
+
+    for copy in head_copies + attend_copies + project_copies + sums_copies + down_copies:
+        copy.wait_send()
+    for offset in range(1, ranks):
+        normed_copy(offset).wait_send()
+
+    @pl.when(s != t)
+    def _():
+        normed_copy(0).wait_send()
+        last_copy.wait_send()
+
+    def drain(chunk, carry):
+        for way in range(2):
+            place = s if way == 0 else stages - 1 - s
+
+            @pl.when(place > 0)
+            def _():
+                remote(
+                    hidden_out.at[way, chunk],
+                    hidden_in.at[way, chunk],
+                    hidden_send.at[way, chunk],
+                    hidden_recv.at[way, chunk],
+                    t,
+                    s + (-1 if way == 0 else 1),
+                ).wait_send()
+
+            @pl.when(place < stages - 1)
+            def _():
+                active_copy(way, chunk).wait_send()
+
+        return carry
+
+    lax.fori_loop(0, chunks, drain, 0)
+
+
+def stationary(ranks, stages, *operands):
+    query_rows, _, _, residual, _, out_weight, up_weight, down_weight = operands
+    members = ranks * stages
+    batches, few_tokens, inner = query_rows.shape
+    width = inner // members
+    tokens = few_tokens * members
+    rows = batches * tokens // stages
+    half = rows * stages // 2
+    features = out_weight.shape[0]
+    depth, hidden = up_weight.shape
+    band = BAND
+    chunks = hidden // band
+    bands = (chunks, depth, band)
+    half_type, dma = jnp.bfloat16, pltpu.SemaphoreType.DMA
+    scratch = [
+        pltpu.VMEM(out_weight.shape, half_type),
+        pltpu.VMEM(bands, half_type),
+        pltpu.VMEM(bands, half_type),
+        pltpu.VMEM((3, members, batches, few_tokens, width), half_type),
+        pltpu.VMEM((ranks, batches, tokens, width), half_type),
+        pltpu.VMEM((batches, tokens, features), jnp.float32),
+        pltpu.VMEM((stages - 1, rows, features), half_type),
+        pltpu.VMEM((stages - 1, rows, features), half_type),
+        pltpu.VMEM((rows, features), jnp.float32),
+        pltpu.VMEM((ranks, rows, 128), jnp.float32),
+        pltpu.VMEM((rows, features), half_type),
+        pltpu.VMEM((2 * half, depth), half_type),
+        pltpu.VMEM((2, chunks, half, band), half_type),
+        pltpu.VMEM((2, chunks, half, band), half_type),
+        pltpu.VMEM((2, chunks, half, band), half_type),
+        pltpu.VMEM((2 * half, depth), jnp.float32),
+        pltpu.VMEM((ranks - 1, rows, depth), half_type),
+        pltpu.VMEM((ranks - 1, rows, depth), half_type),
+        pltpu.VMEM((rows, depth), half_type),
+        pltpu.VMEM((rows, depth), half_type),
+        dma,
+        dma((2, chunks)),
+        dma((3,)),
+        dma((3, members - 1)),
+        dma((3, members - 1)),
+        dma((batches, ranks - 1)),
+        dma((batches, ranks - 1)),
+        dma((stages - 1,)),
+        dma((stages - 1,)),
+        dma((ranks - 1,)),
+        dma((ranks - 1,)),
+        dma((ranks,)),
+        dma((stages,)),
+        dma((2, chunks)),
+        dma((2, chunks)),
+        dma((2, chunks)),
+        dma((2, chunks)),
+        dma((ranks - 1,)),
+        dma((ranks - 1,)),
+        dma,
+        dma,
+    ]
+    vmem = pl.BlockSpec(memory_space=pltpu.VMEM)
+    return pl.pallas_call(
+        functools.partial(block_kernel, ranks, stages, chunks),
+        out_shape=jax.ShapeDtypeStruct(residual.shape, half_type),
+        in_specs=[vmem] * 5 + [pl.BlockSpec(memory_space=pl.ANY)] * 3,
+        out_specs=vmem,
+        scratch_shapes=scratch,
+        compiler_params=pltpu.CompilerParams(
+            collective_id=0, has_side_effects=True, vmem_limit_bytes=40 * 1024 * 1024
+        ),
+    )(*operands)
+
+
 def solution(mesh):
     in_specs = (
         P("groups", ("sp", "tp"), None),
@@ -135,4 +625,14 @@
         P("sp", "tp"),
     )
     out_specs = P("groups", "sp", "tp")
-    return jax.shard_map(body, mesh=mesh, in_specs=in_specs, out_specs=out_specs, check_vma=False)
+    def block(*operands):
+        sizes = mesh.shape
+        rows = operands[0].shape[0] * operands[0].shape[1] * sizes["sp"] * sizes["tp"]
+        square = sizes["sp"] == sizes["tp"]
+        whole_heads = operands[0].shape[2] % (sizes["sp"] * sizes["tp"] * HEAD_FEATURES) == 0
+        few = operands[6].shape[1] % BAND == 0 and rows < operands[6].shape[0]
+        if square and whole_heads and few:
+            return stationary(sizes["tp"], sizes["sp"], *operands)
+        return body(*operands)
+
+    return jax.shard_map(block, mesh=mesh, in_specs=in_specs, out_specs=out_specs, check_vma=False)

time: 487 us -> 108 us (0.22)
  waiting for transfers between devices: 366 us -> 0 us
  Pallas kernels: 0 us -> 98.5 us
  blocking collectives: 34.5 us -> 0 us
  local copies, waits for them, and re-layouts: 31.7 us -> 9.55 us
  starting transfers between devices: 22.1 us -> 0 us
  matrix products: 15.7 us -> 0 us
  between operations: 13.3 us -> 0.02 us
    all_gather x3 -> x0, waiting for transfers between devices: 333 us -> none  [the longest x1 162 us: body(): lax.all_gather(down_weight, 'sp', axis=0, tiled=True)]
    pallas_call x0 -> x1, Pallas kernels: none -> 98.5 us  [stationary(): pl.pallas_call(functools.partial(block_kernel, ranks, stages, chunks), ou...]
    all_gather x4 -> x0, blocking collectives: 27.6 us -> none  [the longest x1 7.28 us: attend(): lax.all_gather(value_heads, 'tp', axis=1, tiled=True)]
    unnamed x5 -> x0, waiting for transfers between devices: 24.7 us -> none
    all_to_all x4 -> x0, starting transfers between devices: 22 us -> none  [the longest x1 6.6 us: attend(): lax.all_to_all(query_part, 'sp', split_axis=2, concat_axis=1, tiled=True)]
    unnamed x22 -> x17, local copies, waits for them, and re-layouts: 26.3 us -> 9.55 us
    dot_general x4 -> x0, matrix products: 15.7 us -> none  [the longest x2 15 us: contract_last(): lax.dot_general(left, right, (((1,), (1,)), ((), ())), preferred_element_...]
    all_to_all x4 -> x0, waiting for transfers between devices: 8.16 us -> none  [the longest x1 5.97 us: attend(): lax.all_to_all(ordered, 'sp', split_axis=1, concat_axis=2, tiled=True)]
  transfers between devices with their start and end apart: 8 -> 0, of which waited for: 6 -> 0; matrix products, arithmetic and copies ran while one was open for 7% -> 0% of each run, Pallas kernels for 0% -> 0%
where the time goes in v2:
time: 108 us
  Pallas kernels  98.5 us (91%)
  local copies, waits for them, and re-layouts  9.55 us (9%)
    pallas_call x1, Pallas kernels, stationary(): pl.pallas_call(functools.partial(block_kernel, ranks, stages, chunks), ou...  98.5 us
    unnamed x17, local copies, waits for them, and re-layouts  9.55 us

profile of v2, /device:TPU:16, one launch (start us, length us, event | category | flops | bytes accessed | tf_op | source)
XLA Modules:
  0.0 108.1 jit_solution(4956336967529203974)
XLA Ops:
  0.0 0.0 copy-start
  0.0 1.6 %copy-done = bf16[640,1792]{1,0:T(8,128)(2,1)S(1)} copy-done((bf16[640,1792]{1,0:T(8,128)(2,1)S(1)}, bf16[640,1792]{1,0:T(8,128)(2,1)}, u32[]{:S(2)}) %copy-start) | copy-done | bytes 2293784
  1.6 0.0 copy-start.1
  1.6 1.6 %copy-done.1 = bf16[640,1792]{1,0:T(8,128)(2,1)S(1)} copy-done((bf16[640,1792]{1,0:T(8,128)(2,1)S(1)}, bf16[640,1792]{1,0:T(8,128)(2,1)}, u32[]{:S(2)}) %copy-start.1) | copy-done | bytes 2293784
  3.3 0.0 copy-start.2
  3.3 1.3 %copy-done.2 = bf16[640,1024]{1,0:T(8,128)(2,1)S(1)} copy-done((bf16[640,1024]{1,0:T(8,128)(2,1)S(1)}, bf16[640,1024]{1,0:T(8,128)(2,1)}, u32[]{:S(2)}) %copy-start.2) | copy-done | bytes 1310744
  4.6 0.0 copy-start.3
  4.6 0.9 copy-done.3
  5.5 0.0 copy-start.4
  5.5 0.9 copy-done.4
  6.4 0.0 copy-start.5
  6.4 0.9 copy-done.5
  7.3 0.0 copy-start.6
  7.3 0.9 copy-done.6
  8.2 0.0 copy-start.7
  8.2 0.7 copy-done.7
  8.9 98.5 %shard_map.82 = bf16[2,32,640]{2,1,0:T(8,128)(2,1)S(1)} custom-call(bf16[2,8,4096]{2,1,0:T(8,128)(2,1)S(1)} %copy-done.3, bf16[2,8,4096]{2,1,0:T(8,128)(2,1)S(1)} %copy-done.4, bf16[2,8,4096]{2,1,0:T(8,128)(2,1)S(1)} %copy-done.5, bf16[2,32,640]{2,1,0:T(8,128)(2,1)S(1)} %copy-done.6, f32[4,640]{1,0:T(4,128)S(1)} %copy-done.7, ...), custom_call_target="tpu_custom_call" | custom-call | tf_op jit(solution)/shard_map/pallas_call | solution.py:604
  107.4 0.6 copy.10
Async XLA Ops:
  0.0 1.6 %copy-start = (bf16[640,1792]{1,0:T(8,128)(2,1)S(1)}, bf16[640,1792]{1,0:T(8,128)(2,1)}, u32[]{:S(2)}) copy-start(bf16[640,1792]{1,0:T(8,128)(2,1)} %up_hbm.1) | copy-start | bytes 6881284
  1.6 1.6 %copy-start.1 = (bf16[640,1792]{1,0:T(8,128)(2,1)S(1)}, bf16[640,1792]{1,0:T(8,128)(2,1)}, u32[]{:S(2)}) copy-start(bf16[640,1792]{1,0:T(8,128)(2,1)} %down_hbm.1) | copy-start | bytes 6881284
  3.3 1.3 %copy-start.2 = (bf16[640,1024]{1,0:T(8,128)(2,1)S(1)}, bf16[640,1024]{1,0:T(8,128)(2,1)}, u32[]{:S(2)}) copy-start(bf16[640,1024]{1,0:T(8,128)(2,1)} %out_hbm.1) | copy-start | bytes 3932164
  4.6 0.9 copy-start.3
  5.5 0.9 copy-start.4
  6.4 0.9 copy-start.5
  7.3 0.9 copy-start.6
  8.2 0.7 copy-start.7

commit v3 on v2

--- a/solution.py
+++ b/solution.py
@@ -131,15 +131,20 @@
     ranks,
     stages,
     chunks,
+    query_hbm,
+    key_hbm,
+    value_hbm,
+    residual_hbm,
+    modulation_hbm,
+    out_hbm,
+    up_hbm,
+    down_hbm,
+    result_ref,
     query_ref,
     key_ref,
     value_ref,
     residual_ref,
     modulation_ref,
-    out_hbm,
-    up_hbm,
-    down_hbm,
-    result_ref,
     out_weight,
     up_weight,
     down_weight,
@@ -160,6 +165,7 @@
     down_in,
     last_out,
     last_in,
+    input_sem,
     out_sem,
     weight_sem,
     own_sem,
@@ -173,6 +179,7 @@
     sums_recv,
     normed_send,
     normed_recv,
+    relay_send,
     hidden_send,
     hidden_recv,
     active_send,
@@ -185,6 +192,10 @@
     t, s = lax.axis_index("tp"), lax.axis_index("sp")
     members = ranks * stages
     me = s * ranks + t
+    core = lax.rem(t, 2)
+    chip = lax.div(t, 2)
+    chips = ranks // 2
+    sibling = t + 1 - 2 * core
     batches, few_tokens, _ = query_ref.shape
     width = heads.shape[-1]
     tokens = members * few_tokens
@@ -203,6 +214,20 @@
             device_id_type=pl.DeviceIdType.MESH,
         )
 
+    input_copies = [
+        pltpu.make_async_copy(source, target, input_sem.at[at])
+        for at, (source, target) in enumerate(
+            (
+                (query_hbm, query_ref),
+                (key_hbm, key_ref),
+                (value_hbm, value_ref),
+                (residual_hbm, residual_ref),
+                (modulation_hbm, modulation_ref),
+            )
+        )
+    ]
+    for copy in input_copies:
+        copy.start()
     out_copy = pltpu.make_async_copy(out_hbm, out_weight, out_sem)
     up_copies, down_copies_in = (
         [
@@ -227,6 +252,8 @@
             device_id={"tp": lax.rem(other, ranks), "sp": lax.div(other, ranks)},
             device_id_type=pl.DeviceIdType.MESH,
         )
+    for copy in input_copies:
+        copy.wait()
     pl.semaphore_wait(barrier, members - 1)
 
     def head_copy(at, source, offset):
@@ -266,6 +293,16 @@
         return loaded.reshape(tokens, HEAD_FEATURES).astype(jnp.bfloat16)
 
     score_scale = 1.0 / math.sqrt(HEAD_FEATURES)
+    def attend_copy(batch, source, at, rank):
+        return remote(
+            attended.at[source, batch],
+            attended.at[source, batch],
+            attend_send.at[batch, at],
+            attend_recv.at[batch, source],
+            rank,
+            s,
+        )
+
     attend_copies = []
     for batch in range(batches):
         for head in range(width // HEAD_FEATURES):
@@ -281,21 +318,24 @@
                 preferred_element_type=jnp.float32,
             )
             attended[t, batch, :, columns] = (weighted / row_total).astype(jnp.bfloat16)
-        for offset in range(1, ranks):
-            copy = remote(
-                attended.at[t, batch],
-                attended.at[t, batch],
-                attend_send.at[batch, offset - 1],
-                attend_recv.at[batch, offset - 1],
-                lax.rem(t + offset, ranks),
-                s,
-            )
+        for offset in range(chips):
+            rank = lax.rem(t + 2 * offset, ranks) if offset else sibling
+            copy = attend_copy(batch, t, offset, rank)
             copy.start()
             attend_copies.append(copy)
 
     out_copy.wait()
-    for copy in attend_copies:
-        copy.wait_recv()
+    for batch in range(batches):
+        for offset in range(1, chips):
+            source = lax.rem(t + ranks - 2 * offset, ranks)
+            copy = attend_copy(batch, source, chips - 1 + offset, sibling)
+            copy.wait_recv()
+            copy.start()
+            attend_copies.append(copy)
+    for batch in range(batches):
+        for offset in range(chips):
+            source = lax.rem(sibling + ranks - 2 * offset, ranks)
+            attend_copy(batch, source, 0, sibling).wait_recv()
     total = None
     for rank in range(ranks):
         left = attended[rank].reshape(batches * tokens, width)
@@ -357,6 +397,7 @@
     normed_out[...] = normed_rows
 
     own_rows = pl.ds(pl.multiple_of(s * rows, rows), rows)
+    own_core = lax.rem(s, 2)
 
     def normed_copy(offset):
         return remote(
@@ -364,11 +405,15 @@
             normed.at[own_rows],
             normed_send.at[offset],
             normed_recv.at[s],
-            lax.rem(t + offset, ranks),
+            2 * lax.rem(chip + offset, chips) + own_core,
             t,
         )
 
-    for offset in range(1, ranks):
+    def relay_copy(at, source):
+        block = normed.at[pl.ds(pl.multiple_of(source * rows, rows), rows)]
+        return remote(block, block, relay_send.at[at], normed_recv.at[source], sibling, s)
+
+    for offset in range(1, chips):
         normed_copy(offset).start()
 
     @pl.when(s != t)
@@ -379,21 +424,18 @@
     def _():
         normed[own_rows, :] = normed_rows
 
+    relays = [relay_copy(at, 2 * at + core) for at in range(stages // 2)]
+    for at, relay in enumerate(relays):
+
+        @pl.when(jnp.logical_or(t != s, s != 2 * at + core))
+        def _():
+            relay.wait_recv()
+
+        relay.start()
+    for at in range(stages // 2):
+        relay_copy(at, 2 * at + 1 - core).wait_recv()
     for copy in up_copies:
         copy.wait()
-    for stage in range(stages):
-
-        @pl.when(jnp.logical_or(t != s, s != stage))
-        def _():
-            remote(
-                normed_out,
-                normed.at[pl.ds(stage * rows, rows)],
-                normed_send.at[0],
-                normed_recv.at[stage],
-                t,
-                s,
-            ).wait_recv()
-
     for copy in down_copies_in:
         copy.wait()
     down_total[...] = jnp.zeros_like(down_total)
@@ -511,8 +553,10 @@
 
     for copy in head_copies + attend_copies + project_copies + sums_copies + down_copies:
         copy.wait_send()
-    for offset in range(1, ranks):
+    for offset in range(1, chips):
         normed_copy(offset).wait_send()
+    for relay in relays:
+        relay.wait_send()
 
     @pl.when(s != t)
     def _():
@@ -558,6 +602,7 @@
     bands = (chunks, depth, band)
     half_type, dma = jnp.bfloat16, pltpu.SemaphoreType.DMA
     scratch = [
+        *(pltpu.VMEM(operand.shape, operand.dtype) for operand in operands[:5]),
         pltpu.VMEM(out_weight.shape, half_type),
         pltpu.VMEM(bands, half_type),
         pltpu.VMEM(bands, half_type),
@@ -578,19 +623,21 @@
         pltpu.VMEM((ranks - 1, rows, depth), half_type),
         pltpu.VMEM((rows, depth), half_type),
         pltpu.VMEM((rows, depth), half_type),
+        dma((5,)),
         dma,
         dma((2, chunks)),
         dma((3,)),
         dma((3, members - 1)),
         dma((3, members - 1)),
         dma((batches, ranks - 1)),
-        dma((batches, ranks - 1)),
+        dma((batches, ranks)),
         dma((stages - 1,)),
         dma((stages - 1,)),
         dma((ranks - 1,)),
         dma((ranks - 1,)),
-        dma((ranks,)),
+        dma((ranks // 2,)),
         dma((stages,)),
+        dma((stages // 2,)),
         dma((2, chunks)),
         dma((2, chunks)),
         dma((2, chunks)),
@@ -604,11 +651,11 @@
     return pl.pallas_call(
         functools.partial(block_kernel, ranks, stages, chunks),
         out_shape=jax.ShapeDtypeStruct(residual.shape, half_type),
-        in_specs=[vmem] * 5 + [pl.BlockSpec(memory_space=pl.ANY)] * 3,
+        in_specs=[pl.BlockSpec(memory_space=pl.ANY)] * 8,
         out_specs=vmem,
         scratch_shapes=scratch,
         compiler_params=pltpu.CompilerParams(
-            collective_id=0, has_side_effects=True, vmem_limit_bytes=40 * 1024 * 1024
+            collective_id=0, has_side_effects=True, vmem_limit_bytes=62 * 1024 * 1024
         ),
     )(*operands)
 
@@ -628,7 +675,7 @@
     def block(*operands):
         sizes = mesh.shape
         rows = operands[0].shape[0] * operands[0].shape[1] * sizes["sp"] * sizes["tp"]
-        square = sizes["sp"] == sizes["tp"]
+        square = sizes["sp"] == sizes["tp"] and sizes["sp"] % 2 == 0
         whole_heads = operands[0].shape[2] % (sizes["sp"] * sizes["tp"] * HEAD_FEATURES) == 0
         few = operands[6].shape[1] % BAND == 0 and rows < operands[6].shape[0]
         if square and whole_heads and few:

time: 108 us -> 94.3 us (0.87)
  local copies, waits for them, and re-layouts: 9.55 us -> 1.53 us
  Pallas kernels: 98.5 us -> 92.6 us
    unnamed x17 -> x1, local copies, waits for them, and re-layouts: 9.55 us -> 1.53 us
    pallas_call x1, Pallas kernels: 98.5 us -> 92.6 us  [stationary(): pl.pallas_call(functools.partial(block_kernel, ranks, stages, chunks), ou...]
where the time goes in v3:
time: 94.3 us; the launch traced here: 94.2 us
  Pallas kernels  92.6 us (98%)
  local copies, waits for them, and re-layouts  1.53 us (2%)
    pallas_call x1, Pallas kernels, stationary(): pl.pallas_call(functools.partial(block_kernel, ranks, stages, chunks), ou...  92.6 us

profile of v3, /device:TPU:16, one launch (start us, length us, event | category | flops | bytes accessed | tf_op | source)
XLA Modules:
  0.0 94.2 jit_solution(12018584443457765777)
XLA Ops:
  0.0 92.6 %shard_map.82 = bf16[2,32,640]{2,1,0:T(8,128)(2,1)} custom-call(bf16[2,8,4096]{2,1,0:T(8,128)(2,1)} %query_hbm.1, bf16[2,8,4096]{2,1,0:T(8,128)(2,1)} %key_hbm.1, bf16[2,8,4096]{2,1,0:T(8,128)(2,1)} %value_hbm.1, bf16[2,32,640]{2,1,0:T(8,128)(2,1)} %residual_hbm.1, f32[4,640]{1,0:T(4,128)} %modulation_hbm.1, bf16[640,1024]{1,0:T(8,128)(2,1)} %out_hbm.1, ...), custom_call_target="tpu_custom_call" | custom-call | tf_op jit(solution)/shard_map/pallas_call | solution.py:651
  92.7 1.5 %copy.10 = bf16[2,32,640]{2,1,0:T(8,128)(2,1)} copy(bf16[2,32,640]{2,1,0:T(8,128)(2,1)} %shard_map.82) | data formatting | bytes 163840

commit v4 on v3

--- a/solution.py
+++ b/solution.py
@@ -10,7 +10,8 @@
 
 D = 2560
 HEAD_FEATURES = 128
-BAND = 256
+BAND = 128
+LAG = 5
 
 
 def contract_last(left, right):
@@ -157,6 +158,7 @@
     sums,
     normed_out,
     normed,
+    hidden_own,
     hidden_out,
     hidden_in,
     active,
@@ -201,7 +203,7 @@
     tokens = members * few_tokens
     part = tokens // stages
     rows = batches * part
-    half = rows * stages // 2
+    half = tokens
     band = hidden_in.shape[-1]
 
     def remote(source, target, send, recv, rank, stage):
@@ -256,40 +258,42 @@
         copy.wait()
     pl.semaphore_wait(barrier, members - 1)
 
-    def head_copy(at, source, offset):
+    def head_copy(batch, at, source, offset):
         other = lax.rem(me + offset, members)
         columns = pl.ds(pl.multiple_of(other * width, width), width)
         return remote(
-            source.at[:, :, columns],
-            heads.at[at, me],
-            head_send.at[at, offset - 1],
-            head_recv.at[at, offset - 1],
+            source.at[batch, :, columns],
+            heads.at[at, batch, me],
+            head_send.at[batch, at, offset - 1],
+            head_recv.at[batch, at, offset - 1],
             lax.rem(other, ranks),
             lax.div(other, ranks),
         )
 
     sources = (query_ref, key_ref, value_ref)
     head_copies = [
-        head_copy(at, source, offset)
-        for offset in range(1, members)
+        [
+            head_copy(batch, at, source, offset)
+            for offset in range(1, members)
+            for at, source in enumerate(sources)
+        ]
+        for batch in range(batches)
+    ]
+    own_columns = pl.ds(pl.multiple_of(me * width, width), width)
+    own_copies = [
+        pltpu.make_async_copy(
+            source.at[batch, :, own_columns], heads.at[at, batch, me], own_sem.at[batch, at]
+        )
+        for batch in range(batches)
         for at, source in enumerate(sources)
     ]
-    for copy in head_copies:
-        copy.start()
-    own_columns = pl.ds(pl.multiple_of(me * width, width), width)
-    own_copies = [
-        pltpu.make_async_copy(source.at[:, :, own_columns], heads.at[at, me], own_sem.at[at])
-        for at, source in enumerate(sources)
-    ]
-    for copy in own_copies:
+    for copy in head_copies[0] + head_copies[1] + own_copies:
         copy.start()
     for copy in own_copies:
         copy.wait()
-    for copy in head_copies:
-        copy.wait_recv()
 
     def head_rows(at, batch, columns):
-        loaded = heads[at, :, batch, :, columns].astype(jnp.float32)
+        loaded = heads[at, batch, :, :, columns].astype(jnp.float32)
         return loaded.reshape(tokens, HEAD_FEATURES).astype(jnp.bfloat16)
 
     score_scale = 1.0 / math.sqrt(HEAD_FEATURES)
@@ -305,6 +309,8 @@
 
     attend_copies = []
     for batch in range(batches):
+        for copy in head_copies[batch]:
+            copy.wait_recv()
         for head in range(width // HEAD_FEATURES):
             columns = slice(head * HEAD_FEATURES, (head + 1) * HEAD_FEATURES)
             scores = score_scale * contract_last(
@@ -325,6 +331,7 @@
             attend_copies.append(copy)
 
     out_copy.wait()
+    project_copies = []
     for batch in range(batches):
         for offset in range(1, chips):
             source = lax.rem(t + ranks - 2 * offset, ranks)
@@ -332,179 +339,114 @@
             copy.wait_recv()
             copy.start()
             attend_copies.append(copy)
-    for batch in range(batches):
         for offset in range(chips):
             source = lax.rem(sibling + ranks - 2 * offset, ranks)
             attend_copy(batch, source, 0, sibling).wait_recv()
-    total = None
-    for rank in range(ranks):
-        left = attended[rank].reshape(batches * tokens, width)
-        product = contract_last(left, out_weight[:, rank * width : (rank + 1) * width])
-        total = product if total is None else total + product
-    projected[...] = total.reshape(projected.shape)
-
-    project_copies = []
-    for offset in range(1, stages):
-        stage = lax.rem(s + offset, stages)
-        block = projected[:, pl.ds(pl.multiple_of(stage * part, part), part), :]
-        outgoing[offset - 1] = block.reshape(rows, -1).astype(jnp.bfloat16)
-        copy = remote(
-            outgoing.at[offset - 1],
-            incoming.at[offset - 1],
-            project_send.at[offset - 1],
-            project_recv.at[offset - 1],
-            t,
-            stage,
-        )
-        copy.start()
-        project_copies.append(copy)
-    kept = projected[:, pl.ds(pl.multiple_of(s * part, part), part), :].reshape(rows, -1)
-    for offset in range(1, stages):
-        project_copies[offset - 1].wait_recv()
-        kept = kept + incoming[offset - 1].astype(jnp.float32)
-    stream = residual_ref[...].astype(jnp.float32).reshape(rows, -1)
-    stream = stream + modulation_ref[0:1, :] * kept
-    mixed[...] = stream
-    first = jnp.sum(stream, axis=1, keepdims=True)
-    second = jnp.sum(stream * stream, axis=1, keepdims=True)
-    lanes = lax.broadcasted_iota(jnp.int32, (rows, 128), 1)
-    sums[t] = jnp.where(lanes == 0, first, second)
+        total = None
+        for rank in range(ranks):
+            columns = slice(rank * width, (rank + 1) * width)
+            product = contract_last(attended[rank, batch], out_weight[:, columns])
+            total = product if total is None else total + product
+        projected[batch] = total
+        for offset in range(1, stages):
+            stage = lax.rem(s + offset, stages)
+            block = projected[batch, pl.ds(pl.multiple_of(stage * part, part), part), :]
+            outgoing[batch, offset - 1] = block.astype(jnp.bfloat16)
+            copy = remote(
+                outgoing.at[batch, offset - 1],
+                incoming.at[batch, offset - 1],
+                project_send.at[batch, offset - 1],
+                project_recv.at[batch, offset - 1],
+                t,
+                stage,
+            )
+            copy.start()
+            project_copies.append(copy)
+
     sums_copies = []
-    for offset in range(1, ranks):
-        copy = remote(
-            sums.at[t],
-            sums.at[t],
-            sums_send.at[offset - 1],
-            sums_recv.at[offset - 1],
-            lax.rem(t + offset, ranks),
-            s,
-        )
-        copy.start()
-        sums_copies.append(copy)
-    for copy in sums_copies:
-        copy.wait_recv()
-    both_sums = sums[0]
-    for rank in range(1, ranks):
-        both_sums = both_sums + sums[rank]
-    row_mean = both_sums[:, 0:1] / D
-    spread = both_sums[:, 1:2] / D - row_mean * row_mean
-    normed_rows = (
-        (mixed[...] - row_mean)
-        * lax.rsqrt(spread + 1e-06)
-        * (1.0 + modulation_ref[2:3, :])
-        + modulation_ref[1:2, :]
-    ).astype(jnp.bfloat16)
-    normed_out[...] = normed_rows
-
-    own_rows = pl.ds(pl.multiple_of(s * rows, rows), rows)
+    lanes = lax.broadcasted_iota(jnp.int32, (part, 128), 1)
+    for batch in range(batches):
+        kept = projected[batch, pl.ds(pl.multiple_of(s * part, part), part), :]
+        for offset in range(1, stages):
+            project_copies[batch * (stages - 1) + offset - 1].wait_recv()
+            kept = kept + incoming[batch, offset - 1].astype(jnp.float32)
+        stream = residual_ref[batch].astype(jnp.float32) + modulation_ref[0:1, :] * kept
+        mixed[batch] = stream
+        first = jnp.sum(stream, axis=1, keepdims=True)
+        second = jnp.sum(stream * stream, axis=1, keepdims=True)
+        sums[batch, t] = jnp.where(lanes == 0, first, second)
+        for offset in range(1, ranks):
+            copy = remote(
+                sums.at[batch, t],
+                sums.at[batch, t],
+                sums_send.at[batch, offset - 1],
+                sums_recv.at[batch, offset - 1],
+                lax.rem(t + offset, ranks),
+                s,
+            )
+            copy.start()
+            sums_copies.append(copy)
+
     own_core = lax.rem(s, 2)
 
-    def normed_copy(offset):
+    def normed_copy(batch, offset):
         return remote(
-            normed_out,
-            normed.at[own_rows],
-            normed_send.at[offset],
-            normed_recv.at[s],
+            normed_out.at[batch],
+            normed.at[batch, s],
+            normed_send.at[batch, offset],
+            normed_recv.at[batch, s],
             2 * lax.rem(chip + offset, chips) + own_core,
             t,
         )
 
-    def relay_copy(at, source):
-        block = normed.at[pl.ds(pl.multiple_of(source * rows, rows), rows)]
-        return remote(block, block, relay_send.at[at], normed_recv.at[source], sibling, s)
-
-    for offset in range(1, chips):
-        normed_copy(offset).start()
-
-    @pl.when(s != t)
-    def _():
-        normed_copy(0).start()
-
-    @pl.when(s == t)
-    def _():
-        normed[own_rows, :] = normed_rows
-
-    relays = [relay_copy(at, 2 * at + core) for at in range(stages // 2)]
-    for at, relay in enumerate(relays):
-
-        @pl.when(jnp.logical_or(t != s, s != 2 * at + core))
+    def relay_copy(batch, at, source):
+        block = normed.at[batch, source]
+        return remote(
+            block, block, relay_send.at[batch, at], normed_recv.at[batch, source], sibling, s
+        )
+
+    for batch in range(batches):
+        for copy in sums_copies[batch * (ranks - 1) : (batch + 1) * (ranks - 1)]:
+            copy.wait_recv()
+        both_sums = sums[batch, 0]
+        for rank in range(1, ranks):
+            both_sums = both_sums + sums[batch, rank]
+        row_mean = both_sums[:, 0:1] / D
+        spread = both_sums[:, 1:2] / D - row_mean * row_mean
+        normed_rows = (
+            (mixed[batch] - row_mean)
+            * lax.rsqrt(spread + 1e-06)
+            * (1.0 + modulation_ref[2:3, :])
+            + modulation_ref[1:2, :]
+        ).astype(jnp.bfloat16)
+        normed_out[batch] = normed_rows
+        for offset in range(1, chips):
+            normed_copy(batch, offset).start()
+
+        @pl.when(s != t)
         def _():
-            relay.wait_recv()
-
-        relay.start()
-    for at in range(stages // 2):
-        relay_copy(at, 2 * at + 1 - core).wait_recv()
+            normed_copy(batch, 0).start()
+
+        @pl.when(s == t)
+        def _():
+            normed[batch, s] = normed_rows
+
+    relays = []
+    for batch in range(batches):
+        for at in range(stages // 2):
+            relay = relay_copy(batch, at, 2 * at + core)
+
+            @pl.when(jnp.logical_or(t != s, s != 2 * at + core))
+            def _():
+                relay.wait_recv()
+
+            relay.start()
+            relays.append(relay)
+    for batch in range(batches):
+        for at in range(stages // 2):
+            relay_copy(batch, at, 2 * at + 1 - core).wait_recv()
     for copy in up_copies:
         copy.wait()
-    for copy in down_copies_in:
-        copy.wait()
-    down_total[...] = jnp.zeros_like(down_total)
-
-    def absorb(way, chunk):
-        block = contract_last(active[way, chunk], down_weight[chunk])
-        down_total[way * half : (way + 1) * half, :] += block
-
-    def slot(at, carry):
-        for way in range(2):
-            place = s if way == 0 else stages - 1 - s
-            toward = -1 if way == 0 else 1
-            chunk = at - (stages - 1 - place)
-
-            @pl.when(jnp.logical_and(chunk >= 0, chunk < chunks))
-            def _():
-                partial = jnp.dot(
-                    normed[way * half : (way + 1) * half, :],
-                    up_weight[chunk],
-                    preferred_element_type=jnp.float32,
-                )
-                hidden_out[way, chunk] = partial.astype(jnp.bfloat16)
-
-                def hidden_copy():
-                    return remote(
-                        hidden_out.at[way, chunk],
-                        hidden_in.at[way, chunk],
-                        hidden_send.at[way, chunk],
-                        hidden_recv.at[way, chunk],
-                        t,
-                        s + toward,
-                    )
-
-                @pl.when(place == stages - 1)
-                def _():
-                    hidden_copy().start()
-
-                @pl.when(place < stages - 1)
-                def _():
-                    hidden_copy().wait_recv()
-                    combined = partial + hidden_in[way, chunk].astype(jnp.float32)
-
-                    @pl.when(place > 0)
-                    def _():
-                        hidden_out[way, chunk] = combined.astype(jnp.bfloat16)
-                        hidden_copy().start()
-
-                    @pl.when(place == 0)
-                    def _():
-                        active[way, chunk] = jax.nn.gelu(combined, approximate=True).astype(
-                            jnp.bfloat16
-                        )
-                        active_copy(way, chunk).start()
-                        absorb(way, chunk)
-
-            back = at - (stages - 1) - place
-
-            @pl.when(jnp.logical_and(place > 0, jnp.logical_and(back >= 0, back < chunks)))
-            def _():
-                active_copy(way, back).wait_recv()
-
-                @pl.when(place < stages - 1)
-                def _():
-                    active_copy(way, back).start()
-
-                absorb(way, back)
-
-        return carry
-
     def active_copy(way, chunk):
         return remote(
             active.at[way, chunk],
@@ -515,53 +457,145 @@
             s + (1 if way == 0 else -1),
         )
 
-    lax.fori_loop(0, chunks + 2 * (stages - 1), slot, 0)
-
-    down_copies = []
-    for offset in range(1, ranks):
-        rank = lax.rem(t + offset, ranks)
-        block = down_total[pl.ds(pl.multiple_of(rank * rows, rows), rows), :]
-        down_out[offset - 1] = block.astype(jnp.bfloat16)
-        copy = remote(
-            down_out.at[offset - 1],
-            down_in.at[offset - 1],
-            down_send.at[offset - 1],
-            down_recv.at[offset - 1],
-            rank,
+    def hidden_copy(way, chunk):
+        return remote(
+            hidden_out.at[way, chunk],
+            hidden_in.at[way, chunk],
+            hidden_send.at[way, chunk],
+            hidden_recv.at[way, chunk],
+            t,
+            s + (-1 if way == 0 else 1),
+        )
+
+    def slot(at, carry):
+        @pl.when(at < chunks)
+        def _():
+            product = jnp.dot(
+                normed[...].reshape(2 * half, -1),
+                up_weight[at],
+                preferred_element_type=jnp.float32,
+            )
+            hidden_own[at] = product
+            for way in range(2):
+
+                @pl.when((s if way == 0 else stages - 1 - s) == stages - 1)
+                def _():
+                    block = product[way * half : (way + 1) * half, :]
+                    hidden_out[way, at] = block.astype(jnp.bfloat16)
+                    hidden_copy(way, at).start()
+
+        for way in range(2):
+            place = s if way == 0 else stages - 1 - s
+            chunk = at - LAG * (stages - 1 - place)
+
+            @pl.when(
+                jnp.logical_and(
+                    place < stages - 1, jnp.logical_and(chunk >= 0, chunk < chunks)
+                )
+            )
+            def _():
+                hidden_copy(way, chunk).wait_recv()
+                combined = hidden_own[chunk, way * half : (way + 1) * half, :]
+                combined = combined + hidden_in[way, chunk].astype(jnp.float32)
+
+                @pl.when(place > 0)
+                def _():
+                    hidden_out[way, chunk] = combined.astype(jnp.bfloat16)
+                    hidden_copy(way, chunk).start()
+
+                @pl.when(place == 0)
+                def _():
+                    active[way, chunk] = jax.nn.gelu(combined, approximate=True).astype(
+                        jnp.bfloat16
+                    )
+                    active_copy(way, chunk).start()
+
+            back = at - LAG * (stages - 1 + place)
+
+            @pl.when(jnp.logical_and(place > 0, jnp.logical_and(back >= 0, back < chunks)))
+            def _():
+                active_copy(way, back).wait_recv()
+
+                @pl.when(place < stages - 1)
+                def _():
+                    active_copy(way, back).start()
+
+            @pl.when(at == chunks - 1 + LAG * (stages - 1 + place))
+            def _():
+                finish(way)
+
+        return carry
+
+    def down_copy(way, offset):
+        return remote(
+            down_out.at[way, offset - 1],
+            down_in.at[way, offset - 1],
+            down_send.at[way, offset - 1],
+            down_recv.at[way, offset - 1],
+            lax.rem(t + offset, ranks),
             s,
         )
-        copy.start()
-        down_copies.append(copy)
-    summed = down_total[pl.ds(pl.multiple_of(t * rows, rows), rows), :]
-    for offset in range(1, ranks):
-        down_copies[offset - 1].wait_recv()
-        summed = summed + down_in[offset - 1].astype(jnp.float32)
-    last_out[...] = summed.astype(jnp.bfloat16)
-    last_copy = remote(last_out, last_in, last_send, last_recv, s, t)
-
-    @pl.when(s != t)
-    def _():
-        last_copy.start()
-        last_copy.wait_recv()
-
-    @pl.when(s == t)
-    def _():
-        last_in[...] = last_out[...]
-
-    result = mixed[...] + modulation_ref[3:4, :] * last_in[...].astype(jnp.float32)
-    result_ref[...] = result.astype(jnp.bfloat16).reshape(result_ref.shape)
-
-    for copy in head_copies + attend_copies + project_copies + sums_copies + down_copies:
+
+    def finish(way):
+        total = None
+        for chunk in range(chunks):
+            product = contract_last(active[way, chunk], down_weight[chunk])
+            total = product if total is None else total + product
+        down_total[way] = total
+        for offset in range(1, ranks):
+            rank = lax.rem(t + offset, ranks)
+            block = down_total[way, pl.ds(pl.multiple_of(rank * part, part), part), :]
+            down_out[way, offset - 1] = block.astype(jnp.bfloat16)
+            down_copy(way, offset).start()
+
+    for copy in down_copies_in:
+        copy.wait()
+    lax.fori_loop(0, chunks + 2 * LAG * (stages - 1), slot, 0)
+
+
+    def last_copy(way):
+        return remote(
+            last_out.at[way], last_in.at[way], last_send.at[way], last_recv.at[way], s, t
+        )
+
+    for way in range(2):
+        summed = down_total[way, pl.ds(pl.multiple_of(t * part, part), part), :]
+        for offset in range(1, ranks):
+            down_copy(way, offset).wait_recv()
+            summed = summed + down_in[way, offset - 1].astype(jnp.float32)
+        last_out[way] = summed.astype(jnp.bfloat16)
+
+        @pl.when(s != t)
+        def _():
+            last_copy(way).start()
+
+        @pl.when(s == t)
+        def _():
+            last_in[way] = last_out[way]
+
+    for way in range(2):
+
+        @pl.when(s != t)
+        def _():
+            last_copy(way).wait_recv()
+
+        result = mixed[way] + modulation_ref[3:4, :] * last_in[way].astype(jnp.float32)
+        result_ref[way] = result.astype(jnp.bfloat16)
+
+    for copy in head_copies[0] + head_copies[1] + attend_copies + project_copies + sums_copies:
         copy.wait_send()
-    for offset in range(1, chips):
-        normed_copy(offset).wait_send()
     for relay in relays:
         relay.wait_send()
-
-    @pl.when(s != t)
-    def _():
-        normed_copy(0).wait_send()
-        last_copy.wait_send()
+    for batch in range(batches):
+        for offset in range(1, chips):
+            normed_copy(batch, offset).wait_send()
+        for offset in range(1, ranks):
+            down_copy(batch, offset).wait_send()
+
+        @pl.when(s != t)
+        def _():
+            normed_copy(batch, 0).wait_send()
+            last_copy(batch).wait_send()
 
     def drain(chunk, carry):
         for way in range(2):
@@ -569,14 +603,7 @@
 
             @pl.when(place > 0)
             def _():
-                remote(
-                    hidden_out.at[way, chunk],
-                    hidden_in.at[way, chunk],
-                    hidden_send.at[way, chunk],
-                    hidden_recv.at[way, chunk],
-                    t,
-                    s + (-1 if way == 0 else 1),
-                ).wait_send()
+                hidden_copy(way, chunk).wait_send()
 
             @pl.when(place < stages - 1)
             def _():
@@ -593,8 +620,7 @@
     batches, few_tokens, inner = query_rows.shape
     width = inner // members
     tokens = few_tokens * members
-    rows = batches * tokens // stages
-    half = rows * stages // 2
+    part = tokens // stages
     features = out_weight.shape[0]
     depth, hidden = up_weight.shape
     band = BAND
@@ -606,46 +632,47 @@
         pltpu.VMEM(out_weight.shape, half_type),
         pltpu.VMEM(bands, half_type),
         pltpu.VMEM(bands, half_type),
-        pltpu.VMEM((3, members, batches, few_tokens, width), half_type),
+        pltpu.VMEM((3, batches, members, few_tokens, width), half_type),
         pltpu.VMEM((ranks, batches, tokens, width), half_type),
         pltpu.VMEM((batches, tokens, features), jnp.float32),
-        pltpu.VMEM((stages - 1, rows, features), half_type),
-        pltpu.VMEM((stages - 1, rows, features), half_type),
-        pltpu.VMEM((rows, features), jnp.float32),
-        pltpu.VMEM((ranks, rows, 128), jnp.float32),
-        pltpu.VMEM((rows, features), half_type),
-        pltpu.VMEM((2 * half, depth), half_type),
-        pltpu.VMEM((2, chunks, half, band), half_type),
-        pltpu.VMEM((2, chunks, half, band), half_type),
-        pltpu.VMEM((2, chunks, half, band), half_type),
-        pltpu.VMEM((2 * half, depth), jnp.float32),
-        pltpu.VMEM((ranks - 1, rows, depth), half_type),
-        pltpu.VMEM((ranks - 1, rows, depth), half_type),
-        pltpu.VMEM((rows, depth), half_type),
-        pltpu.VMEM((rows, depth), half_type),
+        pltpu.VMEM((batches, stages - 1, part, features), half_type),
+        pltpu.VMEM((batches, stages - 1, part, features), half_type),
+        pltpu.VMEM((batches, part, features), jnp.float32),
+        pltpu.VMEM((batches, ranks, part, 128), jnp.float32),
+        pltpu.VMEM((batches, part, features), half_type),
+        pltpu.VMEM((batches, stages, part, depth), half_type),
+        pltpu.VMEM((chunks, 2 * tokens, band), jnp.float32),
+        pltpu.VMEM((2, chunks, tokens, band), half_type),
+        pltpu.VMEM((2, chunks, tokens, band), half_type),
+        pltpu.VMEM((2, chunks, tokens, band), half_type),
+        pltpu.VMEM((batches, tokens, depth), jnp.float32),
+        pltpu.VMEM((batches, ranks - 1, part, depth), half_type),
+        pltpu.VMEM((batches, ranks - 1, part, depth), half_type),
+        pltpu.VMEM((batches, part, depth), half_type),
+        pltpu.VMEM((batches, part, depth), half_type),
         dma((5,)),
         dma,
         dma((2, chunks)),
-        dma((3,)),
-        dma((3, members - 1)),
-        dma((3, members - 1)),
+        dma((batches, 3)),
+        dma((batches, 3, members - 1)),
+        dma((batches, 3, members - 1)),
         dma((batches, ranks - 1)),
         dma((batches, ranks)),
-        dma((stages - 1,)),
-        dma((stages - 1,)),
-        dma((ranks - 1,)),
-        dma((ranks - 1,)),
-        dma((ranks // 2,)),
-        dma((stages,)),
-        dma((stages // 2,)),
+        dma((batches, stages - 1)),
+        dma((batches, stages - 1)),
+        dma((batches, ranks - 1)),
+        dma((batches, ranks - 1)),
+        dma((batches, ranks // 2)),
+        dma((batches, stages)),
+        dma((batches, stages // 2)),
         dma((2, chunks)),
         dma((2, chunks)),
         dma((2, chunks)),
         dma((2, chunks)),
-        dma((ranks - 1,)),
-        dma((ranks - 1,)),
-        dma,
-        dma,
+        dma((batches, ranks - 1)),
+        dma((batches, ranks - 1)),
+        dma((batches,)),
+        dma((batches,)),
     ]
     vmem = pl.BlockSpec(memory_space=pltpu.VMEM)
     return pl.pallas_call(
@@ -678,7 +705,7 @@
         square = sizes["sp"] == sizes["tp"] and sizes["sp"] % 2 == 0
         whole_heads = operands[0].shape[2] % (sizes["sp"] * sizes["tp"] * HEAD_FEATURES) == 0
         few = operands[6].shape[1] % BAND == 0 and rows < operands[6].shape[0]
-        if square and whole_heads and few:
+        if square and whole_heads and few and operands[0].shape[0] == 2:
             return stationary(sizes["tp"], sizes["sp"], *operands)
         return body(*operands)
 

time: 94.3 us -> 81 us (0.86)
  Pallas kernels: 92.6 us -> 79.4 us
    pallas_call x1, Pallas kernels: 92.6 us -> 79.4 us  [stationary(): pl.pallas_call(functools.partial(block_kernel, ranks, stages, chunks), ou...]
where the time goes in v4:
time: 81 us; the launch traced here: 80.9 us
  Pallas kernels  79.4 us (98%)
  local copies, waits for them, and re-layouts  1.53 us (2%)
    pallas_call x1, Pallas kernels, stationary(): pl.pallas_call(functools.partial(block_kernel, ranks, stages, chunks), ou...  79.4 us

profile of v4, /device:TPU:16, one launch (start us, length us, event | category | flops | bytes accessed | tf_op | source)
XLA Modules:
  0.0 80.9 jit_solution(12713739626776025252)
XLA Ops:
  0.0 79.4 %shard_map.82 = bf16[2,32,640]{2,1,0:T(8,128)(2,1)} custom-call(bf16[2,8,4096]{2,1,0:T(8,128)(2,1)} %query_hbm.1, bf16[2,8,4096]{2,1,0:T(8,128)(2,1)} %key_hbm.1, bf16[2,8,4096]{2,1,0:T(8,128)(2,1)} %value_hbm.1, bf16[2,32,640]{2,1,0:T(8,128)(2,1)} %residual_hbm.1, f32[4,640]{1,0:T(4,128)} %modulation_hbm.1, bf16[640,1024]{1,0:T(8,128)(2,1)} %out_hbm.1, ...), custom_call_target="tpu_custom_call" | custom-call | tf_op jit(solution)/shard_map/pallas_call | solution.py:678
  79.4 1.5 %copy.10 = bf16[2,32,640]{2,1,0:T(8,128)(2,1)} copy(bf16[2,32,640]{2,1,0:T(8,128)(2,1)} %shard_map.82) | data formatting | bytes 163840

commit v5 on v4

--- a/solution.py
+++ b/solution.py
@@ -242,8 +242,6 @@
         ]
         for at, (source, target) in enumerate(((up_hbm, up_weight), (down_hbm, down_weight)))
     )
-    for copy in [out_copy, *up_copies, *down_copies_in]:
-        copy.start()
 
     barrier = pltpu.get_barrier_semaphore()
     for offset in range(1, members):
@@ -288,6 +286,8 @@
         for at, source in enumerate(sources)
     ]
     for copy in head_copies[0] + head_copies[1] + own_copies:
+        copy.start()
+    for copy in [out_copy, *up_copies, *down_copies_in]:
         copy.start()
     for copy in own_copies:
         copy.wait()
@@ -520,6 +520,10 @@
                 def _():
                     active_copy(way, back).start()
 
+            @pl.when(at == early - 1 + LAG * (stages - 1 + place))
+            def _():
+                down_total[way] = down_product(way, 0, early)
+
             @pl.when(at == chunks - 1 + LAG * (stages - 1 + place))
             def _():
                 finish(way)
@@ -536,12 +540,17 @@
             s,
         )
 
-    def finish(way):
+    early = chunks - chunks // 4
+
+    def down_product(way, low, high):
         total = None
-        for chunk in range(chunks):
+        for chunk in range(low, high):
             product = contract_last(active[way, chunk], down_weight[chunk])
             total = product if total is None else total + product
-        down_total[way] = total
+        return total
+
+    def finish(way):
+        down_total[way] += down_product(way, early, chunks)
         for offset in range(1, ranks):
             rank = lax.rem(t + offset, ranks)
             block = down_total[way, pl.ds(pl.multiple_of(rank * part, part), part), :]
@@ -704,7 +713,7 @@
         rows = operands[0].shape[0] * operands[0].shape[1] * sizes["sp"] * sizes["tp"]
         square = sizes["sp"] == sizes["tp"] and sizes["sp"] % 2 == 0
         whole_heads = operands[0].shape[2] % (sizes["sp"] * sizes["tp"] * HEAD_FEATURES) == 0
-        few = operands[6].shape[1] % BAND == 0 and rows < operands[6].shape[0]
+        few = operands[6].shape[1] >= 4 * BAND and operands[6].shape[1] % BAND == 0 and rows < operands[6].shape[0]
         if square and whole_heads and few and operands[0].shape[0] == 2:
             return stationary(sizes["tp"], sizes["sp"], *operands)
         return body(*operands)

time: 81 us -> 79.6 us (0.983)
  Pallas kernels: 79.4 us -> 77.2 us
    pallas_call x1, Pallas kernels: 79.4 us -> 77.2 us  [stationary(): pl.pallas_call(functools.partial(block_kernel, ranks, stages, chunks), ou...]
where the time goes in v5:
time: 79.6 us; the launch traced here: 78.7 us
  Pallas kernels  77.2 us (97%)
  local copies, waits for them, and re-layouts  1.53 us (2%)
    pallas_call x1, Pallas kernels, stationary(): pl.pallas_call(functools.partial(block_kernel, ranks, stages, chunks), ou...  77.2 us

profile of v5, /device:TPU:16, one launch (start us, length us, event | category | flops | bytes accessed | tf_op | source)
XLA Modules:
  0.0 78.7 jit_solution(5944268718179924449)
XLA Ops:
  0.0 77.2 %shard_map.82 = bf16[2,32,640]{2,1,0:T(8,128)(2,1)} custom-call(bf16[2,8,4096]{2,1,0:T(8,128)(2,1)} %query_hbm.1, bf16[2,8,4096]{2,1,0:T(8,128)(2,1)} %key_hbm.1, bf16[2,8,4096]{2,1,0:T(8,128)(2,1)} %value_hbm.1, bf16[2,32,640]{2,1,0:T(8,128)(2,1)} %residual_hbm.1, f32[4,640]{1,0:T(4,128)} %modulation_hbm.1, bf16[640,1024]{1,0:T(8,128)(2,1)} %out_hbm.1, ...), custom_call_target="tpu_custom_call" | custom-call | tf_op jit(solution)/shard_map/pallas_call | solution.py:687
  77.2 1.5 %copy.10 = bf16[2,32,640]{2,1,0:T(8,128)(2,1)} copy(bf16[2,32,640]{2,1,0:T(8,128)(2,1)} %shard_map.82) | data formatting | bytes 163840
